TPU v7x, 32 devices: a whole 2x2x4 slice. The times are simulated.
32 devices in a mesh: frames: 8 (over y, x, core), pix: 4 (over z).
Axes of the slice: x: 2, y: 2, z: 4, core: 2. Of those that a mesh axis runs over, the one named last changes fastest.
Arguments:
- edge_frames: int32 [2, 1536], P(None, 'frames'), may hold values from 0 to 127, as said below
- rotvec: float32 [3, 128], replicated, may hold values from -0.06 to 0.06
- trans: float32 [3, 128], replicated, may hold values from -0.15 to 0.15
- inv_depth: float32 [128, 3072], P('frames', 'pix'), may hold values from 0.2 to 1
- depth_damping: float32 [128, 3072], P('frames', 'pix'), may hold values from 0.01 to 0.1
- flow: float32 [1536, 2, 3072], P('frames', None, 'pix'), may hold values from -0.3 to 0.3
- weight: float32 [1536, 2, 3072], P('frames', None, 'pix'), may hold values from 0.02 to 1
- mask: int32 [1536, 3072], P('frames', 'pix'), may hold values 0 or 1
Outputs:
- pose_step: float32 [6, 128], P(None, 'frames')
- depth_step: float32 [128, 3072], P('frames', 'pix')
Inputs may be any that keep to these rules, and one draw needn't show every extreme that they name: Edge e of the block of 192 edges held by one index of frames has its target edge_frames[1, e] among that index's 16 keyframes; its source edge_frames[0, e] differs from the target by 1 to 8, and in every block some source lies exactly 8 away.
All inputs are finite; a program needn't handle non-finite values. No bound on the sum of `mask` on one device may be relied on, other than what follows from the above.
Results may differ from a plain program's by a relative error of at most 0.00015.
Values sent between devices are 32-bit elements; how exact they have to be, the bound alone decides.
A program may use at most 64 MiB of HBM per device.

v0:
```python
import functools
import jax
import jax.numpy as jnp
from jax import lax
from jax.experimental import pallas as pl
from jax.experimental.pallas import tpu as pltpu
from jax.sharding import PartitionSpec as P

ROWS = 48
COLS = 64
RADIUS = 8
ITERS = 6
REG = 100.0
F32 = jnp.float32
BF16 = jnp.bfloat16
L = 128
WIN = 32
SLOT = 24
VMEM_LIMIT = 60 * 1024 * 1024
UPPER = [(i, j) for i in range(6) for j in range(i, 6) if (i, j) != (0, 1)]


def split(x):
    high = x.astype(BF16)
    return high, (x - high.astype(F32)).astype(BF16)


def iota(shape, dim):
    return lax.broadcasted_iota(jnp.int32, shape, dim)


def aggregate(dest_ref, flow_ref, weight_ref, mask_ref, own_ref, low_ref, high_ref):
    edges = dest_ref.shape[1]
    tiles = mask_ref.shape[1] // L
    own = own_ref.shape[1]
    side = low_ref.shape[1]
    rows = own + 2 * side
    pick = (iota((rows, edges), 0) == dest_ref[...]).astype(F32).astype(BF16)
    for tile in range(tiles):
        cols = slice(tile * L, (tile + 1) * L)
        live = mask_ref[:, cols].astype(F32)
        fields = []
        for comp in range(2):
            take = pl.ds(tile * 2 + comp, edges, stride=2 * tiles)
            conf = weight_ref[take, :] * live
            fields += [conf, conf * flow_ref[take, :]]
        high, low = split(jnp.concatenate(fields, axis=1))
        out = jnp.dot(pick, high, preferred_element_type=F32) + jnp.dot(
            pick, low, preferred_element_type=F32
        )
        for field in range(4):
            part = out[:, field * L : (field + 1) * L]
            own_ref[field, :, cols] = part[:own]
            low_ref[field, :, cols] = part[own : own + side]
            high_ref[field, :, cols] = part[own + side :]


def jac_sums(u, v, uu, vv, uv, ds, a, b):
    return [
        ds * a,
        ds * b,
        -ds * (u * a + v * b),
        -uv * a - vv * b,
        uu * a + uv * b,
        u * b - v * a,
    ]


def adj_t(rel, cor, vec):
    out = []
    for j in range(3):
        out.append(rel[j] * vec[0] + rel[3 + j] * vec[1] + rel[6 + j] * vec[2])
    for j in range(3):
        out.append(
            cor[j] * vec[0]
            + cor[3 + j] * vec[1]
            + cor[6 + j] * vec[2]
            + rel[j] * vec[3]
            + rel[3 + j] * vec[4]
            + rel[6 + j] * vec[5]
        )
    return out


def build(
    first_ref, pose_ref, own_ref, low_ref, high_ref, depth_ref, damp_ref,
    matrix_ref, zh_ref, zl_ref, base_ref, scale_ref,
    frame_ref, pair_ref, hacc, racc, hc, rc, adc, wide, depth3, damp3,
):
    f_dev, pix = depth_ref.shape
    tiles = pix // L
    half = f_dev // 2
    ox, oy, oz = pose_ref[0], pose_ref[1], pose_ref[2]
    zero = jnp.zeros_like(ox)
    cross = [[zero, -oz, oy], [oz, zero, -ox], [-oy, ox, zero]]
    sq = ox * ox + oy * oy + oz * oz
    c1 = 1.0 - sq / 6.0 + sq * sq / 120.0
    c2 = 0.5 - sq / 24.0 + sq * sq / 720.0
    for r in range(3):
        for c in range(3):
            square = cross[r][0] * cross[0][c] + cross[r][1] * cross[1][c] + cross[r][2] * cross[2][c]
            frame_ref[3 * r + c] = float(r == c) + c1 * cross[r][c] + c2 * square
        frame_ref[9 + r] = pose_ref[3 + r]
    for tile in range(tiles):
        depth3[tile] = depth_ref[:, tile * L : (tile + 1) * L]
        damp3[tile] = damp_ref[:, tile * L : (tile + 1) * L]
    hc[...] = jnp.zeros_like(hc)
    rc[...] = jnp.zeros_like(rc)
    adc[...] = jnp.zeros_like(adc)
    lane = iota((SLOT, L), 1)
    row = iota((SLOT, L), 0)
    row8 = iota((8, L), 0)

    for part in range(2):
        base = part * half
        win = slice(base, base + SLOT)
        if part == 0:
            pad = lambda x: jnp.concatenate([x, jnp.zeros((WIN - SLOT, L), F32)], axis=0)
        else:
            pad = lambda x: jnp.concatenate([jnp.zeros((WIN - SLOT, L), F32), x], axis=0)

        @pl.loop(0, half)
        def per_source(i):
            s = i + base
            here = [frame_ref[k, pl.ds(s + RADIUS, 1), :] for k in range(12)]
            there = [frame_ref[k, win, :] for k in range(12)]
            rel = [
                there[3 * r] * here[3 * c]
                + there[3 * r + 1] * here[3 * c + 1]
                + there[3 * r + 2] * here[3 * c + 2]
                for r in range(3)
                for c in range(3)
            ]
            tr = [
                there[9 + r]
                - (rel[3 * r] * here[9] + rel[3 * r + 1] * here[10] + rel[3 * r + 2] * here[11])
                for r in range(3)
            ]
            cor = []
            for c in range(3):
                cor.append(tr[1] * rel[6 + c] - tr[2] * rel[3 + c])
            for c in range(3):
                cor.append(tr[2] * rel[c] - tr[0] * rel[6 + c])
            for c in range(3):
                cor.append(tr[0] * rel[3 + c] - tr[1] * rel[c])
            at = lane == s + RADIUS
            for k in range(9):
                pair_ref[k] = rel[k]
                pair_ref[12 + k] = cor[k]
                adc[k, win, :] = jnp.where(at, rel[k], adc[k, win, :])
                adc[9 + k, win, :] = jnp.where(at, cor[k], adc[9 + k, win, :])
            for k in range(3):
                pair_ref[9 + k] = tr[k]
            hacc[...] = jnp.zeros_like(hacc)
            racc[...] = jnp.zeros_like(racc)
            if part == 0:
                slot = jnp.where(i == 0, 4, jnp.where(i <= 4, i - 1, 7 - i))
                shift = jnp.where(i > 4, i, 0)
                keep = row8 >= i
            else:
                slot = jnp.where(i <= 3, i, jnp.where(i == 7, 4, 6 - i))
                shift = jnp.where((i > 3) & (i < 7), i + 1, 0)
                keep = row8 <= i
            is_source = row == s + RADIUS - base

            def per_tile(tile):
                cols = slice(tile * L, (tile + 1) * L)
                fields = []
                for k in range(4):
                    src = high_ref if part == 0 else low_ref
                    got = src[k, pl.ds(pl.multiple_of(slot * 8, 8), 8), cols]
                    got = jnp.where(keep, pltpu.roll(got, shift, 0), 0.0)
                    if part == 0:
                        mine = own_ref[k, pl.ds(pl.multiple_of(s * SLOT + 8, 8), 16), cols]
                        fields.append(jnp.concatenate([got, mine], axis=0))
                    else:
                        mine = own_ref[k, pl.ds(pl.multiple_of(s * SLOT, 8), 16), cols]
                        fields.append(jnp.concatenate([mine, got], axis=0))
                wu, fu, wv, fv = fields
                pixel = first_ref[0] + tile * L + iota((1, L), 1)
                prow = pixel // COLS
                pcol = pixel - prow * COLS
                col = (pcol.astype(F32) - 0.5 * (COLS - 1)) / COLS
                rowc = (prow.astype(F32) - 0.5 * (ROWS - 1)) / COLS
                depth = depth3[tile, pl.ds(s, 1), :]
                m = [pair_ref[k] for k in range(21)]
                point = [
                    m[3 * k] * col + m[3 * k + 1] * rowc + m[3 * k + 2] + depth * m[9 + k]
                    for k in range(3)
                ]
                iz = 1.0 / point[2]
                u = point[0] * iz
                v = point[1] * iz
                ds = depth * iz
                su = iz * (m[9] - u * m[11])
                sv = iz * (m[10] - v * m[11])
                au = wu * su
                av = wv * sv
                gu = wu * (col - u) + fu
                gv = wv * (rowc - v) + fv
                curv = jnp.sum(au * su + av * sv, axis=0, keepdims=True) + damp3[tile, pl.ds(s, 1), :]
                grad = -jnp.sum(su * gu + sv * gv, axis=0, keepdims=True)
                bstep = grad / curv
                scale = 1.0 / jnp.sqrt(curv)
                base_ref[tile, pl.ds(s, 1), :] = bstep
                scale_ref[tile, pl.ds(s, 1), :] = scale
                uu = 1.0 + u * u
                vv = 1.0 + v * v
                uv = u * v
                e = jac_sums(u, v, uu, vv, uv, ds, au, av)
                back = adj_t(m[0:9], m[12:21], e)
                zcols = pl.ds(pl.multiple_of(s * pix + tile * L, L), L)
                for j in range(6):
                    total = -jnp.sum(back[j], axis=0, keepdims=True)
                    full = jnp.where(is_source, total, e[j]) * scale
                    high, low = split(pad(full))
                    zh_ref[j * WIN : (j + 1) * WIN, zcols] = high
                    zl_ref[j * WIN : (j + 1) * WIN, zcols] = low
                r = jac_sums(u, v, uu, vv, uv, ds, -gu - au * bstep, -gv - av * bstep)
                for j in range(6):
                    racc[j] += r[j]
                ju = [ds, None, -ds * u, -uv, uu, -v]
                jv = [None, ds, -ds * v, -vv, uv, u]
                wju = [None if x is None else wu * x for x in ju]
                wjv = [None if x is None else wv * x for x in jv]
                for n, (a, b) in enumerate(UPPER):
                    terms = []
                    if ju[a] is not None and ju[b] is not None:
                        terms.append(wju[a] * ju[b])
                    if jv[a] is not None and jv[b] is not None:
                        terms.append(wjv[a] * jv[b])
                    hacc[n] += terms[0] if len(terms) == 1 else terms[0] + terms[1]

            for tile in range(tiles):
                per_tile(tile)
            for n in range(len(UPPER)):
                hc[n, win, :] = jnp.where(at, jnp.sum(hacc[n], axis=1, keepdims=True), hc[n, win, :])
            for j in range(6):
                rc[j, win, :] = jnp.where(at, jnp.sum(racc[j], axis=1, keepdims=True), rc[j, win, :])

    def accumulate(s, carry):
        hh, hl = carry
        cols = pl.ds(pl.multiple_of(s * pix, L), pix)
        zh = zh_ref[:, cols]
        zl = zl_ref[:, cols]
        nt = (((1,), (1,)), ((), ()))
        return (
            hh + lax.dot_general(zh, zh, nt, preferred_element_type=F32),
            hl + lax.dot_general(zh, zl, nt, preferred_element_type=F32),
        )

    none = jnp.zeros((6 * WIN, 6 * WIN), F32)
    hh, hl = lax.fori_loop(0, f_dev, accumulate, (none, none))

    h = [[None] * 6 for _ in range(6)]
    for n, (a, b) in enumerate(UPPER):
        h[a][b] = hc[n]
        h[b][a] = h[a][b]
    rel = [adc[k] for k in range(9)]
    cor = [adc[9 + k] for k in range(9)]
    ad = [[None] * 6 for _ in range(6)]
    for i in range(3):
        for j in range(3):
            ad[i][j] = rel[3 * i + j]
            ad[i][3 + j] = cor[3 * i + j]
            ad[3 + i][3 + j] = rel[3 * i + j]
    lane = iota((WIN, L), 1)
    row = iota((WIN, L), 0)
    eye = row == lane

    def total(terms):
        out = None
        for x, y in terms:
            if x is None or y is None:
                continue
            out = x * y if out is None else out + x * y
        return out

    had = [[total([(h[i][k], ad[k][j]) for k in range(6)]) for j in range(6)] for i in range(6)]
    wide[...] = jnp.zeros_like(wide)
    matrix_ref[...] = jnp.zeros_like(matrix_ref)
    for i in range(6):
        rows = slice(i * WIN, (i + 1) * WIN)
        for j in range(6):
            cols = slice(j * WIN, (j + 1) * WIN)
            wide[rows, cols] = -had[i][j][:, :WIN]
            both = jnp.sum(total([(ad[k][i], had[k][j]) for k in range(6)]), axis=0, keepdims=True)
            if h[i][j] is not None:
                both = both + jnp.sum(h[i][j], axis=1, keepdims=True)
            diag = jnp.where(eye, both, 0.0)
            matrix_ref[rows, cols] = diag[:, :WIN]
    wide[: 6 * WIN, : 6 * WIN] = wide[: 6 * WIN, : 6 * WIN] - hl
    flipped = wide[...].T
    matrix_ref[: 6 * WIN, : 6 * WIN] = (
        matrix_ref[: 6 * WIN, : 6 * WIN] - hh + wide[: 6 * WIN, : 6 * WIN] + flipped[: 6 * WIN, : 6 * WIN]
    )
    r = [rc[j] for j in range(6)]
    back = adj_t(rel, cor, r)
    for j in range(6):
        here = jnp.sum(jnp.where(eye, jnp.sum(r[j], axis=1, keepdims=True), 0.0) - back[j], axis=0, keepdims=True)
        matrix_ref[6 * WIN : 6 * WIN + 1, j * WIN : (j + 1) * WIN] = here[:, :WIN]


def remote(src, dst, sems, phase, which, axis, peer):
    return pltpu.make_async_remote_copy(
        src_ref=src,
        dst_ref=dst,
        send_sem=sems.at[0, phase, which],
        recv_sem=sems.at[1, phase, which],
        device_id={axis: peer},
        device_id_type=pl.DeviceIdType.MESH,
    )


def peers(axis):
    count = lax.axis_size(axis)
    me = lax.axis_index(axis)
    return [lax.rem(me + step, count) for step in range(1, count)]


def finish(
    matrix_ref, zh_ref, zl_ref, base_ref, scale_ref, pose_ref, step_ref,
    flat, cols_ref, step3, land, summed, rows_ref, pix_sem, round_sem,
):
    count = lax.axis_size("frames")
    me = lax.axis_index("frames")
    f_dev, pix = step_ref.shape
    width = matrix_ref.shape[1]
    size = 6 * WIN
    zcount = lax.axis_size("pix")
    z = lax.axis_index("pix")
    chunk = matrix_ref.shape[0] // zcount

    def piece(which):
        return pl.ds(pl.multiple_of(which * chunk, 8), chunk)

    sent = []
    for peer in peers("pix"):
        copy = remote(matrix_ref.at[piece(peer)], land.at[z], pix_sem, 0, len(sent), "pix", peer)
        copy.start()
        sent.append(copy)
    land[z] = matrix_ref[piece(z), :]
    for copy in sent:
        copy.wait_recv()
    reduced = land[0]
    for k in range(1, zcount):
        reduced = reduced + land[k]
    for copy in sent:
        copy.wait_send()
    summed[piece(z), :] = reduced
    sent = []
    for peer in peers("pix"):
        copy = remote(summed.at[piece(z)], summed.at[piece(z)], pix_sem, 1, len(sent), "pix", peer)
        copy.start()
        sent.append(copy)
    for copy in sent:
        copy.wait_recv()
    for copy in sent:
        copy.wait_send()

    shape = (count, width)
    frame = iota(shape, 1) % WIN
    window = iota(shape, 0)
    below = (frame < f_dev) & (window > 0)
    above = (frame >= WIN - f_dev) & (window < count - 1)
    own = (frame >= RADIUS) & (frame < RADIUS + f_dev)

    def settle(x):
        down = pltpu.roll(pltpu.roll(x, 1, 0), width - f_dev, 1)
        up = pltpu.roll(pltpu.roll(x, count - 1, 0), f_dev, 1)
        return x + jnp.where(below, down, 0.0) + jnp.where(above, up, 0.0)

    def dot(x, y):
        return jnp.sum(jnp.where(own, x * y, 0.0), keepdims=True)

    def gather(step, row):
        rows_ref[step, me] = row
        sent = []
        here = rows_ref.at[step, me]
        for peer in peers("frames"):
            copy = remote(here, here, round_sem, step, len(sent), "frames", peer)
            copy.start()
            sent.append(copy)
        for copy in sent:
            copy.wait_recv()
        for w in range(count):
            flat[w : w + 1, :] = rows_ref[step, w]
        for copy in sent:
            copy.wait_send()
        return settle(flat[0:count, :])

    def product(step, x):
        flat[0:count, :] = x
        cols_ref[...] = jnp.broadcast_to(flat[pl.ds(me, 1), :], (L, width)).T[:size]
        pieces = []
        for lt in range(width // L):
            pieces.append(
                jnp.sum(summed[:size, lt * L : (lt + 1) * L] * cols_ref[...], axis=0, keepdims=True)
            )
        return gather(step, jnp.concatenate(pieces, axis=1)) + REG * x

    residual = gather(0, summed[size : size + 1, :])
    x = jnp.zeros_like(residual)
    direction = residual
    rr = dot(residual, residual)
    for step in range(ITERS):
        image = product(step + 1, direction)
        alpha = rr / dot(direction, image)
        x = x + alpha * direction
        residual = residual - alpha * image
        new = dot(residual, residual)
        direction = residual + (new / rr) * direction
        rr = new
    flat[0:count, :] = x
    mine = flat[pl.ds(me, 1), :]
    pose_ref[...] = jnp.broadcast_to(mine, pose_ref.shape)
    cols_ref[...] = jnp.broadcast_to(mine, (L, width)).T[:size]

    @pl.loop(0, f_dev)
    def per_source(s):
        for tile in range(pix // L):
            zcols = pl.ds(pl.multiple_of(s * pix + tile * L, L), L)
            z = zh_ref[:, zcols].astype(F32) + zl_ref[:, zcols].astype(F32)
            image = jnp.sum(z * cols_ref[...], axis=0, keepdims=True)
            here = (tile, pl.ds(s, 1), slice(None))
            step3[here] = base_ref[here] - scale_ref[here] * image

    for tile in range(pix // L):
        step_ref[:, tile * L : (tile + 1) * L] = step3[tile]


def solve(
    first_ref, dest_ref, flow_ref, weight_ref, mask_ref, pose_ref, depth_ref, damp_ref,
    x_ref, step_ref, own_ref, low_out, high_out, low_ref, high_ref, edge_sem, *scratch,
):
    matrix, zh, zl, base, scale = scratch[:5]
    barrier = pltpu.get_barrier_semaphore()
    total = 0
    for axis in ("frames", "pix"):
        for peer in peers(axis):
            pl.semaphore_signal(
                barrier, inc=1, device_id={axis: peer}, device_id_type=pl.DeviceIdType.MESH
            )
            total += 1
    aggregate(dest_ref, flow_ref, weight_ref, mask_ref, own_ref, low_out, high_out)
    pl.semaphore_wait(barrier, total)
    around = peers("frames")
    edge = [
        remote(low_out, low_ref, edge_sem, 0, 0, "frames", around[-1]),
        remote(high_out, high_ref, edge_sem, 1, 0, "frames", around[0]),
    ]
    for copy in edge:
        copy.start()
    for copy in edge:
        copy.wait()
    build(
        first_ref, pose_ref, own_ref, low_ref, high_ref, depth_ref, damp_ref,
        matrix, zh, zl, base, scale, *scratch[5:15],
    )
    finish(matrix, zh, zl, base, scale, x_ref, step_ref, *scratch[15:])


def call(body, out, scratch, smem, count, **params):
    vm = pl.BlockSpec(memory_space=pltpu.VMEM)
    sm = pl.BlockSpec(memory_space=pltpu.SMEM)
    return pl.pallas_call(
        body,
        out_shape=[jax.ShapeDtypeStruct(s, t) for s, t in out],
        in_specs=[sm] * smem + [vm] * count,
        out_specs=[vm] * len(out),
        scratch_shapes=scratch,
        compiler_params=pltpu.CompilerParams(vmem_limit_bytes=VMEM_LIMIT, **params),
    )


def per_device(edge_frames, rotvec, trans, inv_depth, depth_damping, flow, weight, mask):
    f_dev, pix = inv_depth.shape
    edges = mask.shape[0]
    tiles = pix // L
    me = lax.axis_index("frames")
    start = me * f_dev
    source = edge_frames[0] - start + RADIUS
    target = edge_frames[1] - start + RADIUS
    own_rows = f_dev * SLOT
    side = 40
    s = source - RADIUS
    mine = s * SLOT + target - (s // 8) * 8
    i = source
    q = target - 8
    tile = jnp.where(i <= 3, i, jnp.where(i == 7, 4, 6 - i))
    line = jnp.where((i > 3) & (i < 7), q + 7 - i, q)
    lowest = own_rows + tile * 8 + line
    i = source - f_dev - RADIUS
    q = target - f_dev
    tile = jnp.where(i == 0, 4, jnp.where(i <= 4, i - 1, 7 - i))
    line = jnp.where(i > 4, q - i, q)
    highest = own_rows + side + tile * 8 + line
    dest = jnp.where(source < RADIUS, lowest, jnp.where(source >= RADIUS + f_dev, highest, mine))

    def flat(x):
        return x.reshape(edges, 2, tiles, L).transpose(0, 2, 1, 3).reshape(edges * 2 * tiles, L)

    pose = jnp.pad(jnp.concatenate([rotvec, trans], axis=0), ((0, 0), (RADIUS, RADIUS)))
    pose = lax.dynamic_slice_in_dim(pose, start, WIN, axis=1)
    pose = jnp.broadcast_to(pose[:, :, None], (6, WIN, L))
    first = (lax.axis_index("pix") * pix).reshape(1).astype(jnp.int32)
    n = len(UPPER)
    width = 256
    count = lax.axis_size("frames")
    zcount = lax.axis_size("pix")
    chunk = -(-(6 * WIN + 8) // (8 * zcount)) * 8
    x, step = call(
        solve,
        [((8, width), F32), ((f_dev, pix), F32)],
        [
            pltpu.VMEM((4, own_rows, pix), F32),
            pltpu.VMEM((4, side, pix), F32),
            pltpu.VMEM((4, side, pix), F32),
            pltpu.VMEM((4, side, pix), F32),
            pltpu.VMEM((4, side, pix), F32),
            pltpu.SemaphoreType.DMA((2, 2, 1)),
            pltpu.VMEM((chunk * zcount, width), F32),
            pltpu.VMEM((6 * WIN, f_dev * pix), BF16),
            pltpu.VMEM((6 * WIN, f_dev * pix), BF16),
            pltpu.VMEM((tiles, f_dev, L), F32),
            pltpu.VMEM((tiles, f_dev, L), F32),
            pltpu.VMEM((12, WIN, L), F32),
            pltpu.VMEM((21, SLOT, L), F32),
            pltpu.VMEM((n, SLOT, L), F32),
            pltpu.VMEM((6, SLOT, L), F32),
            pltpu.VMEM((n, WIN, L), F32),
            pltpu.VMEM((6, WIN, L), F32),
            pltpu.VMEM((18, WIN, L), F32),
            pltpu.VMEM((256, 256), F32),
            pltpu.VMEM((tiles, f_dev, L), F32),
            pltpu.VMEM((tiles, f_dev, L), F32),
            pltpu.VMEM((L, width), F32),
            pltpu.VMEM((6 * WIN, L), F32),
            pltpu.VMEM((tiles, f_dev, L), F32),
            pltpu.VMEM((zcount, chunk, width), F32),
            pltpu.VMEM((chunk * zcount, width), F32),
            pltpu.VMEM((ITERS + 1, count, 1, width), F32),
            pltpu.SemaphoreType.DMA((2, 2, zcount)),
            pltpu.SemaphoreType.DMA((2, ITERS + 1, count)),
        ],
        1, 7, collective_id=0, has_side_effects=True,
    )(
        first, dest.reshape(1, edges), flat(flow), flat(weight), mask,
        pose, inv_depth, depth_damping,
    )
    return (x[0].reshape(8, WIN)[:6, RADIUS : RADIUS + f_dev], step)


def solution(mesh):
    return jax.shard_map(
        per_device,
        mesh=mesh,
        in_specs=(
            P(None, "frames"),
            P(),
            P(),
            P("frames", "pix"),
            P("frames", "pix"),
            P("frames", None, "pix"),
            P("frames", None, "pix"),
            P("frames", "pix"),
        ),
        out_specs=(P(None, "frames"), P("frames", "pix")),
        check_vma=False,
    )
```

profile of v0, /device:TPU:1, one launch (start us, length us, event | category | flops | bytes accessed | tf_op | source)
XLA Modules:
  0.0 95.1 jit_solution(10809281883738026195)
XLA Ops:
  0.6 1.3 %compare_select_fusion.6.dest_ref = s32[1,192]{1,0:T(1,128)} fusion(s32[2,192]{1,0:T(2,128)} %param.8, s32[]{:T(128)S(6)} %mul.23), kind=kLoop, calls=%fused_computation.17 | loop fusion | flops 10560 | bytes 2308 | tf_op jit(solution)/shard_map/jit(_where)/select_n | solution.py:498
  2.0 1.3 %copy.12 = f32[192,2,768]{2,0,1:T(8,128)S(1)} copy(f32[192,2,768]{2,1,0:T(2,128)} %param.13) | data formatting | bytes 2359296 | tf_op args[5]
  3.3 0.2 reshape.22
  3.5 0.0 copy-start
  3.5 1.9 %copy.13 = f32[192,6,2,128]{3,2,1,0:T(2,128)} copy(f32[192,6,2,128]{3,1,0,2:T(8,128)S(1)} %bitcast.9) | data formatting | bytes 2359296 | tf_op jit(solution)/shard_map/transpose | solution.py:501
  5.5 0.0 copy-done
  5.5 0.1 copy.14
  5.5 0.2 reshape.24
  5.7 0.0 copy-start.1
  5.7 0.0 copy-start.2
  5.8 2.0 %copy.15 = f32[192,6,2,128]{3,2,1,0:T(2,128)} copy(f32[192,6,2,128]{3,1,0,2:T(8,128)S(1)} %bitcast.10) | data formatting | bytes 2359296 | tf_op jit(solution)/shard_map/transpose | solution.py:501
  7.7 0.0 copy-done.1
  7.7 0.0 copy-done.2
  7.7 0.1 fusion.1
  7.8 0.7 broadcast_in_dim.12.pose_ref
  8.5 83.6 %shard_map.95 = (f32[8,256]{1,0:T(8,128)}, f32[16,768]{1,0:T(8,128)}) custom-call(s32[1]{0:T(128)} %bitcast.first_ref, s32[1,192]{1,0:T(1,128)} %compare_select_fusion.6.dest_ref, f32[2304,128]{1,0:T(8,128)} %bitcast.11, f32[2304,128]{1,0:T(8,128)} %bitcast.12, s32[192,768]{1,0:T(8,128)} %mask_ref.1, f32[6,32,128]{2,1,0:T(8,128)} %broadcast_in_dim.12.pose_ref, ...), custom_call_target="tpu_custom_call" | custom-call | tf_op jit(solution)/shard_map/pallas_call | solution.py:512
  92.2 0.7 slice_reduce_fusion
  92.9 0.1 reshape_squeeze.3
  93.0 0.7 slice.15
  93.6 1.4 %copy.17 = f32[16,768]{1,0:T(8,128)} copy(f32[16,768]{1,0:T(8,128)} %get-tuple-element.9) | data formatting | bytes 98304
Async XLA Ops:
  3.5 1.9 %copy-start = (f32[192,2,768]{2,1,0:T(2,128)S(1)}, f32[192,2,768]{2,1,0:T(2,128)}, u32[]{:S(2)}) copy-start(f32[192,2,768]{2,1,0:T(2,128)} %param.14) | copy-start | bytes 3538948
  5.7 2.0 %copy-start.1 = (f32[3,128]{1,0:T(4,128)S(1)}, f32[3,128]{1,0:T(4,128)}, u32[]{:S(2)}) copy-start(f32[3,128]{1,0:T(4,128)} %param.9) | copy-start | bytes 4612
  5.7 2.0 %copy-start.2 = (f32[3,128]{1,0:T(4,128)S(1)}, f32[3,128]{1,0:T(4,128)}, u32[]{:S(2)}) copy-start(f32[3,128]{1,0:T(4,128)} %param.10) | copy-start | bytes 4612
where the time goes:
time: 95.7 us; the launch traced here: 95.1 us
  Pallas kernels  83.6 us (87%)
  local copies, waits for them, and re-layouts  9.3 us (10%)
  other arithmetic  1.42 us (1%)
    pallas_call x1, Pallas kernels, per_device(): call(solve, [((8, width), F32), ((f_dev, pix), F32)], [pltpu.VMEM((4, own...  83.6 us
    transpose x2, local copies, waits for them, and re-layouts, flat(): x.reshape(edges, 2, tiles, L).transpose(0, 2, 1, 3)  3.89 us
    unnamed x9, local copies, waits for them, and re-layouts  2.87 us

commit v1 on v0

--- a/solution.py
+++ b/solution.py
@@ -16,6 +16,8 @@
 L = 128
 WIN = 32
 SLOT = 24
+BAND = 2 * RADIUS
+PACKED = 160
 VMEM_LIMIT = 60 * 1024 * 1024
 UPPER = [(i, j) for i in range(6) for j in range(i, 6) if (i, j) != (0, 1)]
 
@@ -29,21 +31,55 @@
     return lax.broadcasted_iota(jnp.int32, shape, dim)
 
 
-def aggregate(dest_ref, flow_ref, weight_ref, mask_ref, own_ref, low_ref, high_ref):
-    edges = dest_ref.shape[1]
-    tiles = mask_ref.shape[1] // L
+def destinations(edge_ref, own_rows, side, f_dev, me):
+    start = me * f_dev
+    source = edge_ref[0:1, :] - start + RADIUS
+    target = edge_ref[1:2, :] - start + RADIUS
+    s = source - RADIUS
+    mine = s * SLOT + target - jnp.where(s >= RADIUS, RADIUS, 0)
+    q = target - RADIUS
+    tile = jnp.where(source <= 3, source, jnp.where(source == 7, 4, 6 - source))
+    line = jnp.where((source > 3) & (source < 7), q + 7 - source, q)
+    lowest = own_rows + tile * 8 + line
+    i = source - f_dev - RADIUS
+    q = target - f_dev
+    tile = jnp.where(i == 0, 4, jnp.where(i <= 4, i - 1, 7 - i))
+    line = jnp.where(i > 4, q - i, q)
+    highest = own_rows + side + tile * 8 + line
+    return jnp.where(source < RADIUS, lowest, jnp.where(source >= RADIUS + f_dev, highest, mine))
+
+
+def fetch(flow_ref, weight_ref, mask_ref, flow3, weight3, mask3, sems):
+    out = []
+    for tile in range(flow3.shape[0]):
+        cols = pl.ds(tile * L, L)
+        pairs = [(mask_ref.at[:, cols], mask3.at[tile])]
+        for comp in range(2):
+            pairs.append((weight_ref.at[:, comp, cols], weight3.at[tile, comp]))
+            pairs.append((flow_ref.at[:, comp, cols], flow3.at[tile, comp]))
+        copies = [pltpu.make_async_copy(a, b, sems.at[tile, n]) for n, (a, b) in enumerate(pairs)]
+        for copy in copies:
+            copy.start()
+        out.append(copies)
+    return out
+
+
+def aggregate(edge_ref, loads, flow3, weight3, mask3, own_ref, low_ref, high_ref, me, f_dev):
+    edges = edge_ref.shape[1]
     own = own_ref.shape[1]
     side = low_ref.shape[1]
     rows = own + 2 * side
-    pick = (iota((rows, edges), 0) == dest_ref[...]).astype(F32).astype(BF16)
-    for tile in range(tiles):
+    dest = destinations(edge_ref, own, side, f_dev, me)
+    pick = (iota((rows, edges), 0) == dest).astype(F32).astype(BF16)
+    for tile, copies in enumerate(loads):
         cols = slice(tile * L, (tile + 1) * L)
-        live = mask_ref[:, cols].astype(F32)
+        for copy in copies:
+            copy.wait()
+        live = mask3[tile].astype(F32)
         fields = []
         for comp in range(2):
-            take = pl.ds(tile * 2 + comp, edges, stride=2 * tiles)
-            conf = weight_ref[take, :] * live
-            fields += [conf, conf * flow_ref[take, :]]
+            conf = weight3[tile, comp] * live
+            fields += [conf, conf * flow3[tile, comp]]
         high, low = split(jnp.concatenate(fields, axis=1))
         out = jnp.dot(pick, high, preferred_element_type=F32) + jnp.dot(
             pick, low, preferred_element_type=F32
@@ -53,6 +89,23 @@
             own_ref[field, :, cols] = part[:own]
             low_ref[field, :, cols] = part[own : own + side]
             high_ref[field, :, cols] = part[own + side :]
+
+
+def window(load, me, f_dev, frames):
+    tiles = frames // L
+    first = lax.rem(me * f_dev - RADIUS + frames, frames)
+    tile = first // L
+    back = lax.rem(L - lax.rem(first, L), L)
+    near = pltpu.roll(load(pl.ds(pl.multiple_of(tile * L, L), L)), back, 1)
+    if tiles == 1:
+        return near
+    after = lax.rem(tile + 1, tiles)
+    far = pltpu.roll(load(pl.ds(pl.multiple_of(after * L, L), L)), back, 1)
+    return jnp.where(iota(near.shape, 1) + lax.rem(first, L) < L, near, far)
+
+
+def spread_rows(x):
+    return jnp.concatenate([x, jnp.zeros((L - x.shape[0], L), F32)], axis=0).T
 
 
 def jac_sums(u, v, uu, vv, uv, ds, a, b):
@@ -83,7 +136,7 @@
 
 
 def build(
-    first_ref, pose_ref, own_ref, low_ref, high_ref, depth_ref, damp_ref,
+    first, pose_ref, own_ref, low_ref, high_ref, depth_ref, damp_ref,
     matrix_ref, zh_ref, zl_ref, base_ref, scale_ref,
     frame_ref, pair_ref, hacc, racc, hc, rc, adc, wide, depth3, damp3,
 ):
@@ -177,7 +230,7 @@
                         mine = own_ref[k, pl.ds(pl.multiple_of(s * SLOT, 8), 16), cols]
                         fields.append(jnp.concatenate([mine, got], axis=0))
                 wu, fu, wv, fv = fields
-                pixel = first_ref[0] + tile * L + iota((1, L), 1)
+                pixel = first + tile * L + iota((1, L), 1)
                 prow = pixel // COLS
                 pcol = pixel - prow * COLS
                 col = (pcol.astype(F32) - 0.5 * (COLS - 1)) / COLS
@@ -318,103 +371,240 @@
     return [lax.rem(me + step, count) for step in range(1, count)]
 
 
-def finish(
-    matrix_ref, zh_ref, zl_ref, base_ref, scale_ref, pose_ref, step_ref,
-    flat, cols_ref, step3, land, summed, rows_ref, pix_sem, round_sem,
-):
+def pack(matrix_ref, packed_ref):
+    size = 6 * WIN
+    lane = iota((WIN, L), 1) % WIN
+    row = iota((WIN, L), 0)
+    inside = row + lane < WIN
+    left = iota((BAND, L), 1) < L // 2
+    packed_ref[...] = jnp.zeros_like(packed_ref)
+
+    def skew(x):
+        for bit in (1, 2, 4, 8, 16):
+            x = jnp.where((lane & bit) != 0, pltpu.roll(x, WIN - bit, 0), x)
+        return jnp.where(inside, x, 0.0)
+
+    rest = []
+    for j in range(6):
+        rows = slice(j * WIN, (j + 1) * WIN)
+        main = skew(matrix_ref[rows, :L])
+        packed_ref[j * BAND : (j + 1) * BAND, :] = main[:BAND]
+        packed_ref[6 * BAND + j : 6 * BAND + j + 1, :] = main[BAND : BAND + 1]
+        rest.append(skew(matrix_ref[rows, L:]))
+    base = 6 * BAND + 8
+    for j in range(3):
+        near = rest[j]
+        far = pltpu.roll(rest[j + 3], L // 2, 1)
+        packed_ref[base + j * BAND : base + (j + 1) * BAND, :] = jnp.where(left, near[:BAND], far[:BAND])
+        at = base + 3 * BAND + j
+        packed_ref[at : at + 1, :] = jnp.where(left[:1], near[BAND : BAND + 1], far[BAND : BAND + 1])
+    packed_ref[6 * BAND + 6 : 6 * BAND + 7, :] = matrix_ref[size : size + 1, :L]
+    packed_ref[base + 3 * BAND + 3 : base + 3 * BAND + 4, :] = jnp.where(
+        left[:1], matrix_ref[size : size + 1, L:], 0.0
+    )
+
+
+def exchange(src, dst, sems, phase, axis):
+    sent = []
+    for peer in peers(axis):
+        copy = remote(src(peer), dst, sems, phase, len(sent), axis, peer)
+        copy.start()
+        sent.append(copy)
+    return sent
+
+
+def operator(packed_ref, land, reduced_ref, gathered, diag_ref, ahead_ref, back_ref, far_ref, pix_sem, round_sem, f_dev, frames):
+    zcount = lax.axis_size("pix")
+    z = lax.axis_index("pix")
     count = lax.axis_size("frames")
     me = lax.axis_index("frames")
-    f_dev, pix = step_ref.shape
-    width = matrix_ref.shape[1]
-    size = 6 * WIN
-    zcount = lax.axis_size("pix")
-    z = lax.axis_index("pix")
-    chunk = matrix_ref.shape[0] // zcount
+    chunk = land.shape[1]
+    tiles = frames // L
 
     def piece(which):
         return pl.ds(pl.multiple_of(which * chunk, 8), chunk)
 
-    sent = []
-    for peer in peers("pix"):
-        copy = remote(matrix_ref.at[piece(peer)], land.at[z], pix_sem, 0, len(sent), "pix", peer)
-        copy.start()
-        sent.append(copy)
-    land[z] = matrix_ref[piece(z), :]
+    sent = exchange(lambda peer: packed_ref.at[piece(peer)], land.at[z], pix_sem, 0, "pix")
+    land[z] = packed_ref[piece(z), :]
     for copy in sent:
         copy.wait_recv()
-    reduced = land[0]
+    total = land[0]
     for k in range(1, zcount):
-        reduced = reduced + land[k]
-    for copy in sent:
+        total = total + land[k]
+    reduced_ref[...] = total
+    more = exchange(lambda peer: reduced_ref, gathered.at[me], round_sem, 0, "frames")
+    gathered[me] = total
+    for copy in more:
+        copy.wait_recv()
+    lane = iota((chunk, L), 1)
+    sums = [[None] * tiles for _ in range(4)]
+    for w in range(count):
+        first = (w * f_dev - RADIUS) % frames
+        start = first % L
+        for k in range(4):
+            part = pltpu.roll(gathered[w], (start - WIN * k) % L, 1)
+            spans = [(first // L, start, min(start + WIN, L))]
+            if start + WIN > L:
+                spans.append(((first // L + 1) % tiles, 0, start + WIN - L))
+            for tile, low, high in spans:
+                term = jnp.where((lane >= low) & (lane < high), part, 0.0)
+                sums[k][tile] = term if sums[k][tile] is None else sums[k][tile] + term
+    for k in range(4):
+        for tile in range(tiles):
+            diag_ref[z, k, :, tile * L : (tile + 1) * L] = sums[k][tile]
+    for copy in sent + more:
         copy.wait_send()
-    summed[piece(z), :] = reduced
-    sent = []
-    for peer in peers("pix"):
-        copy = remote(summed.at[piece(z)], summed.at[piece(z)], pix_sem, 1, len(sent), "pix", peer)
-        copy.start()
-        sent.append(copy)
+    sent = exchange(lambda peer: diag_ref.at[z], diag_ref.at[z], pix_sem, 1, "pix")
     for copy in sent:
         copy.wait_recv()
     for copy in sent:
         copy.wait_send()
 
-    shape = (count, width)
-    frame = iota(shape, 1) % WIN
-    window = iota(shape, 0)
-    below = (frame < f_dev) & (window > 0)
-    above = (frame >= WIN - f_dev) & (window < count - 1)
-    own = (frame >= RADIUS) & (frame < RADIUS + f_dev)
-
-    def settle(x):
-        down = pltpu.roll(pltpu.roll(x, 1, 0), width - f_dev, 1)
-        up = pltpu.roll(pltpu.roll(x, count - 1, 0), f_dev, 1)
-        return x + jnp.where(below, down, 0.0) + jnp.where(above, up, 0.0)
+    def block(k, at):
+        return [
+            diag_ref[at // chunk, k, at % chunk : at % chunk + 8, t * L : (t + 1) * L]
+            for t in range(tiles)
+        ]
+
+    def entry(i, j, half):
+        if i < 4:
+            return block(i, BAND * j + 8 * half)
+        return block(i - 4 + 2 * (j // 3), 6 * BAND + 8 + BAND * (j % 3) + 8 * half)
+
+    row = iota((8, L), 0)
+    lanes = iota((8, L), 1)
+
+    def later(x, half):
+        turned = [pltpu.roll(v, 8 * half, 1, stride=1, stride_axis=0) for v in x]
+        if tiles == 1:
+            return turned
+        mine = lanes >= 8 * half + row
+        return [jnp.where(mine, turned[t], turned[t - 1]) for t in range(tiles)]
+
+    def flip(x):
+        for bit in (4, 2, 1):
+            x = jnp.where((row & bit) != 0, pltpu.roll(x, bit, 0), pltpu.roll(x, 8 - bit, 0))
+        return x
+
+    for i in range(6):
+        for j in range(6):
+            for half in range(2):
+                front = entry(i, j, half)
+                moved = later(entry(j, i, half), half)
+                for t in range(tiles):
+                    ahead_ref[i, 2 * j + half, :, t * L : (t + 1) * L] = flip(front[t])
+                    value = jnp.where(row > 0, moved[t], 0.0) if half == 0 else moved[t]
+                    back_ref[i, 2 * j + half, :, t * L : (t + 1) * L] = value
+    edge = 6 * BAND
+    last = edge + 8 + 3 * BAND
+    for i in range(6):
+        if i < 4:
+            ends = block(i, edge)
+        else:
+            near, far = block(i - 4, last), block(i - 2, last)
+            ends = [jnp.where(row < 3, a, pltpu.roll(b, 3, 0)) for a, b in zip(near, far)]
+        for t in range(tiles):
+            far_ref[i, :, t * L : (t + 1) * L] = jnp.where(row < 6, ends[t], 0.0)
+    sources = [block(k, edge) for k in range(4)] + [block(k, last) for k in range(2)]
+    rhs = []
+    for t in range(tiles):
+        out = jnp.zeros((8, L), F32)
+        for i in range(6):
+            at = 6 if i < 4 else 3
+            out = jnp.where(row == i, sources[i][t][at : at + 1, :], out)
+        rhs.append(out)
+    return rhs, later
+
+
+def conjugate(rhs, later, ahead_ref, back_ref, far_ref):
+    tiles = len(rhs)
+    row = iota((8, L), 0)
+    lanes = iota((8, L), 1)
+
+    def sooner(x, half):
+        turned = [pltpu.roll(v, L - 8 * half - 7, 1, stride=1, stride_axis=0) for v in x]
+        if tiles == 1:
+            return turned
+        mine = lanes + 8 * half + 7 - row < L
+        return [jnp.where(mine, turned[t], turned[(t + 1) % tiles]) for t in range(tiles)]
+
+    def moved(x, steps):
+        turned = [pltpu.roll(v, steps % L, 1) for v in x]
+        if tiles == 1:
+            return turned
+        if steps > 0:
+            return [jnp.where(lanes >= steps, turned[t], turned[t - 1]) for t in range(tiles)]
+        return [jnp.where(lanes < L + steps, turned[t], turned[(t + 1) % tiles]) for t in range(tiles)]
 
     def dot(x, y):
-        return jnp.sum(jnp.where(own, x * y, 0.0), keepdims=True)
-
-    def gather(step, row):
-        rows_ref[step, me] = row
-        sent = []
-        here = rows_ref.at[step, me]
-        for peer in peers("frames"):
-            copy = remote(here, here, round_sem, step, len(sent), "frames", peer)
-            copy.start()
-            sent.append(copy)
-        for copy in sent:
-            copy.wait_recv()
-        for w in range(count):
-            flat[w : w + 1, :] = rows_ref[step, w]
-        for copy in sent:
-            copy.wait_send()
-        return settle(flat[0:count, :])
-
-    def product(step, x):
-        flat[0:count, :] = x
-        cols_ref[...] = jnp.broadcast_to(flat[pl.ds(me, 1), :], (L, width)).T[:size]
-        pieces = []
-        for lt in range(width // L):
-            pieces.append(
-                jnp.sum(summed[:size, lt * L : (lt + 1) * L] * cols_ref[...], axis=0, keepdims=True)
-            )
-        return gather(step, jnp.concatenate(pieces, axis=1)) + REG * x
-
-    residual = gather(0, summed[size : size + 1, :])
-    x = jnp.zeros_like(residual)
-    direction = residual
-    rr = dot(residual, residual)
-    for step in range(ITERS):
-        image = product(step + 1, direction)
+        total = x[0] * y[0]
+        for t in range(1, tiles):
+            total = total + x[t] * y[t]
+        return jnp.sum(total, keepdims=True)
+
+    def product(p):
+        ahead = moved(p, -BAND)
+        acc = [[far_ref[i, :, t * L : (t + 1) * L] * ahead[t] for t in range(tiles)] for i in range(6)]
+        tail = [None] * tiles
+        for j in range(6):
+            wide = [jnp.broadcast_to(v[j : j + 1, :], (8, L)) for v in p]
+            for t in range(tiles):
+                term = far_ref[j, :, t * L : (t + 1) * L] * wide[t]
+                tail[t] = term if tail[t] is None else tail[t] + term
+            for half in range(2):
+                plus = sooner(wide, half)
+                minus = later(wide, half)
+                for i in range(6):
+                    for t in range(tiles):
+                        acc[i][t] = (
+                            acc[i][t]
+                            + ahead_ref[i, 2 * j + half, :, t * L : (t + 1) * L] * plus[t]
+                            + back_ref[i, 2 * j + half, :, t * L : (t + 1) * L] * minus[t]
+                        )
+        tail = moved(tail, BAND)
+        out = []
+        for t in range(tiles):
+            y = tail[t] + REG * p[t]
+            for i in range(6):
+                y = y + jnp.where(row == i, jnp.sum(acc[i][t], axis=0, keepdims=True), 0.0)
+            out.append(y)
+        return out
+
+    def step(_, carry):
+        x, residual, direction, rr = carry
+        image = product(direction)
         alpha = rr / dot(direction, image)
-        x = x + alpha * direction
-        residual = residual - alpha * image
+        x = [a + alpha * b for a, b in zip(x, direction)]
+        residual = [a - alpha * b for a, b in zip(residual, image)]
         new = dot(residual, residual)
-        direction = residual + (new / rr) * direction
-        rr = new
-    flat[0:count, :] = x
-    mine = flat[pl.ds(me, 1), :]
-    pose_ref[...] = jnp.broadcast_to(mine, pose_ref.shape)
-    cols_ref[...] = jnp.broadcast_to(mine, (L, width)).T[:size]
+        beta = new / rr
+        direction = [a + beta * b for a, b in zip(residual, direction)]
+        return x, residual, direction, new
+
+    zero = [jnp.zeros((8, L), F32)] * tiles
+    return lax.fori_loop(0, ITERS, step, (zero, rhs, rhs, dot(rhs, rhs)))[0]
+
+
+def finish(
+    matrix_ref, zh_ref, zl_ref, base_ref, scale_ref, pose_ref, step_ref, frames,
+    cols_ref, step3, packed_ref, land, reduced_ref, gathered, diag_ref, ahead_ref, back_ref, far_ref, x_ref,
+    pix_sem, round_sem,
+):
+    me = lax.axis_index("frames")
+    f_dev, pix = step_ref.shape
+    pack(matrix_ref, packed_ref)
+    rhs, later = operator(
+        packed_ref, land, reduced_ref, gathered, diag_ref, ahead_ref, back_ref, far_ref,
+        pix_sem, round_sem, f_dev, frames,
+    )
+    x = conjugate(rhs, later, ahead_ref, back_ref, far_ref)
+    for t, value in enumerate(x):
+        x_ref[:, t * L : (t + 1) * L] = value
+    mine = window(lambda at: x_ref[:, at], me, f_dev, frames)
+    pose_ref[...] = mine[:6, RADIUS : RADIUS + f_dev]
+    turned = spread_rows(mine)
+    for i in range(6):
+        cols_ref[i * WIN : (i + 1) * WIN, :] = jnp.broadcast_to(turned[:WIN, i : i + 1], (WIN, L))
 
     @pl.loop(0, f_dev)
     def per_source(s):
@@ -429,11 +619,59 @@
         step_ref[:, tile * L : (tile + 1) * L] = step3[tile]
 
 
+def swap_edges(low_out, high_out, low_ref, high_ref, sems):
+    count = lax.axis_size("frames")
+    me = lax.axis_index("frames")
+    down = remote(low_out, low_ref, sems, 0, 0, "frames", lax.rem(me + count - 1, count))
+    up = remote(high_out, high_ref, sems, 1, 0, "frames", lax.rem(me + 1, count))
+
+    @pl.when(me > 0)
+    def _():
+        down.start()
+
+    @pl.when(me < count - 1)
+    def _():
+        up.start()
+
+    def receive():
+        @pl.when(me < count - 1)
+        def _():
+            down.wait_recv()
+
+        @pl.when(me == count - 1)
+        def _():
+            low_ref[...] = jnp.zeros_like(low_ref)
+
+        @pl.when(me > 0)
+        def _():
+            up.wait_recv()
+
+        @pl.when(me == 0)
+        def _():
+            high_ref[...] = jnp.zeros_like(high_ref)
+
+    def drain():
+        @pl.when(me > 0)
+        def _():
+            down.wait_send()
+
+        @pl.when(me < count - 1)
+        def _():
+            up.wait_send()
+
+    return receive, drain
+
+
 def solve(
-    first_ref, dest_ref, flow_ref, weight_ref, mask_ref, pose_ref, depth_ref, damp_ref,
-    x_ref, step_ref, own_ref, low_out, high_out, low_ref, high_ref, edge_sem, *scratch,
+    edge_ref, rot_ref, trans_ref, depth_ref, damp_ref, flow_ref, weight_ref, mask_ref,
+    x_ref, step_ref, flow3, weight3, mask3, load_sem, pose_ref,
+    own_ref, low_out, high_out, low_ref, high_ref, edge_sem, *scratch,
 ):
     matrix, zh, zl, base, scale = scratch[:5]
+    me = lax.axis_index("frames")
+    f_dev, pix = depth_ref.shape
+    frames = rot_ref.shape[1]
+    loads = fetch(flow_ref, weight_ref, mask_ref, flow3, weight3, mask3, load_sem)
     barrier = pltpu.get_barrier_semaphore()
     total = 0
     for axis in ("frames", "pix"):
@@ -442,31 +680,31 @@
                 barrier, inc=1, device_id={axis: peer}, device_id_type=pl.DeviceIdType.MESH
             )
             total += 1
-    aggregate(dest_ref, flow_ref, weight_ref, mask_ref, own_ref, low_out, high_out)
+    poses = []
+    for ref in (rot_ref, trans_ref):
+        poses.append(window(lambda at: ref[:, at], me, f_dev, frames))
+    turned = spread_rows(jnp.concatenate(poses, axis=0))
+    for k in range(6):
+        pose_ref[k] = jnp.broadcast_to(turned[:WIN, k : k + 1], (WIN, L))
+    aggregate(edge_ref, loads, flow3, weight3, mask3, own_ref, low_out, high_out, me, f_dev)
     pl.semaphore_wait(barrier, total)
-    around = peers("frames")
-    edge = [
-        remote(low_out, low_ref, edge_sem, 0, 0, "frames", around[-1]),
-        remote(high_out, high_ref, edge_sem, 1, 0, "frames", around[0]),
-    ]
-    for copy in edge:
-        copy.start()
-    for copy in edge:
-        copy.wait()
+    receive, drain = swap_edges(low_out, high_out, low_ref, high_ref, edge_sem)
+    receive()
+    drain()
     build(
-        first_ref, pose_ref, own_ref, low_ref, high_ref, depth_ref, damp_ref,
+        lax.axis_index("pix") * pix, pose_ref, own_ref, low_ref, high_ref, depth_ref, damp_ref,
         matrix, zh, zl, base, scale, *scratch[5:15],
     )
-    finish(matrix, zh, zl, base, scale, x_ref, step_ref, *scratch[15:])
-
-
-def call(body, out, scratch, smem, count, **params):
+    finish(matrix, zh, zl, base, scale, x_ref, step_ref, frames, *scratch[15:])
+
+
+def call(body, out, scratch, vmem, hbm, **params):
     vm = pl.BlockSpec(memory_space=pltpu.VMEM)
-    sm = pl.BlockSpec(memory_space=pltpu.SMEM)
+    far = pl.BlockSpec(memory_space=pl.ANY)
     return pl.pallas_call(
         body,
         out_shape=[jax.ShapeDtypeStruct(s, t) for s, t in out],
-        in_specs=[sm] * smem + [vm] * count,
+        in_specs=[vm] * vmem + [far] * hbm,
         out_specs=[vm] * len(out),
         scratch_shapes=scratch,
         compiler_params=pltpu.CompilerParams(vmem_limit_bytes=VMEM_LIMIT, **params),
@@ -476,50 +714,31 @@
 def per_device(edge_frames, rotvec, trans, inv_depth, depth_damping, flow, weight, mask):
     f_dev, pix = inv_depth.shape
     edges = mask.shape[0]
+    frames = rotvec.shape[1]
     tiles = pix // L
-    me = lax.axis_index("frames")
-    start = me * f_dev
-    source = edge_frames[0] - start + RADIUS
-    target = edge_frames[1] - start + RADIUS
     own_rows = f_dev * SLOT
     side = 40
-    s = source - RADIUS
-    mine = s * SLOT + target - (s // 8) * 8
-    i = source
-    q = target - 8
-    tile = jnp.where(i <= 3, i, jnp.where(i == 7, 4, 6 - i))
-    line = jnp.where((i > 3) & (i < 7), q + 7 - i, q)
-    lowest = own_rows + tile * 8 + line
-    i = source - f_dev - RADIUS
-    q = target - f_dev
-    tile = jnp.where(i == 0, 4, jnp.where(i <= 4, i - 1, 7 - i))
-    line = jnp.where(i > 4, q - i, q)
-    highest = own_rows + side + tile * 8 + line
-    dest = jnp.where(source < RADIUS, lowest, jnp.where(source >= RADIUS + f_dev, highest, mine))
-
-    def flat(x):
-        return x.reshape(edges, 2, tiles, L).transpose(0, 2, 1, 3).reshape(edges * 2 * tiles, L)
-
-    pose = jnp.pad(jnp.concatenate([rotvec, trans], axis=0), ((0, 0), (RADIUS, RADIUS)))
-    pose = lax.dynamic_slice_in_dim(pose, start, WIN, axis=1)
-    pose = jnp.broadcast_to(pose[:, :, None], (6, WIN, L))
-    first = (lax.axis_index("pix") * pix).reshape(1).astype(jnp.int32)
     n = len(UPPER)
     width = 256
     count = lax.axis_size("frames")
     zcount = lax.axis_size("pix")
-    chunk = -(-(6 * WIN + 8) // (8 * zcount)) * 8
+    chunk = -(-PACKED // (8 * zcount)) * 8
     x, step = call(
         solve,
-        [((8, width), F32), ((f_dev, pix), F32)],
+        [((6, f_dev), F32), ((f_dev, pix), F32)],
         [
+            pltpu.VMEM((tiles, 2, edges, L), F32),
+            pltpu.VMEM((tiles, 2, edges, L), F32),
+            pltpu.VMEM((tiles, edges, L), jnp.int32),
+            pltpu.SemaphoreType.DMA((tiles, 5)),
+            pltpu.VMEM((6, WIN, L), F32),
             pltpu.VMEM((4, own_rows, pix), F32),
             pltpu.VMEM((4, side, pix), F32),
             pltpu.VMEM((4, side, pix), F32),
             pltpu.VMEM((4, side, pix), F32),
             pltpu.VMEM((4, side, pix), F32),
             pltpu.SemaphoreType.DMA((2, 2, 1)),
-            pltpu.VMEM((chunk * zcount, width), F32),
+            pltpu.VMEM((6 * WIN + 8, width), F32),
             pltpu.VMEM((6 * WIN, f_dev * pix), BF16),
             pltpu.VMEM((6 * WIN, f_dev * pix), BF16),
             pltpu.VMEM((tiles, f_dev, L), F32),
@@ -534,21 +753,23 @@
             pltpu.VMEM((256, 256), F32),
             pltpu.VMEM((tiles, f_dev, L), F32),
             pltpu.VMEM((tiles, f_dev, L), F32),
-            pltpu.VMEM((L, width), F32),
             pltpu.VMEM((6 * WIN, L), F32),
             pltpu.VMEM((tiles, f_dev, L), F32),
-            pltpu.VMEM((zcount, chunk, width), F32),
-            pltpu.VMEM((chunk * zcount, width), F32),
-            pltpu.VMEM((ITERS + 1, count, 1, width), F32),
+            pltpu.VMEM((chunk * zcount, L), F32),
+            pltpu.VMEM((zcount, chunk, L), F32),
+            pltpu.VMEM((chunk, L), F32),
+            pltpu.VMEM((count, chunk, L), F32),
+            pltpu.VMEM((zcount, 4, chunk, frames), F32),
+            pltpu.VMEM((6, 12, 8, frames), F32),
+            pltpu.VMEM((6, 12, 8, frames), F32),
+            pltpu.VMEM((6, 8, frames), F32),
+            pltpu.VMEM((8, frames), F32),
             pltpu.SemaphoreType.DMA((2, 2, zcount)),
-            pltpu.SemaphoreType.DMA((2, ITERS + 1, count)),
+            pltpu.SemaphoreType.DMA((2, 1, count)),
         ],
-        1, 7, collective_id=0, has_side_effects=True,
-    )(
-        first, dest.reshape(1, edges), flat(flow), flat(weight), mask,
-        pose, inv_depth, depth_damping,
-    )
-    return (x[0].reshape(8, WIN)[:6, RADIUS : RADIUS + f_dev], step)
+        5, 3, collective_id=0, has_side_effects=True,
+    )(edge_frames, rotvec, trans, inv_depth, depth_damping, flow, weight, mask)
+    return x, step
 
 
 def solution(mesh):

time: 95.7 us -> 68.6 us (0.72)
  Pallas kernels: 83.6 us -> 64.5 us
  local copies, waits for them, and re-layouts: 9.3 us -> 2.69 us
  other arithmetic: 1.42 us -> 0 us
    pallas_call x1, Pallas kernels: 83.6 us -> 64.5 us  [per_device(): call(solve, [((6, f_dev), F32), ((f_dev, pix), F32)], [pltpu.VMEM((tiles,...]
    transpose x2 -> x0, local copies, waits for them, and re-layouts: 3.89 us -> none  [flat(): x.reshape(edges, 2, tiles, L).transpose(0, 2, 1, 3)]
    slice x2 -> x0, local copies, waits for them, and re-layouts: 1.38 us -> none  [per_device(): return (x[0].reshape(8, WIN)[:6, RADIUS:RADIUS + f_dev], step)]
    select_n x1 -> x0, other arithmetic: 1.34 us -> none  [per_device(): jnp.where(source < RADIUS, lowest, jnp.where(source >= RADIUS + f_dev, hi...]
    unnamed x9 -> x2, local copies, waits for them, and re-layouts: 2.87 us -> 2.69 us
where the time goes in v1:
time: 68.6 us; the launch traced here: 67.8 us
  Pallas kernels  64.5 us (94%)
  local copies, waits for them, and re-layouts  2.69 us (4%)
    pallas_call x1, Pallas kernels, per_device(): call(solve, [((6, f_dev), F32), ((f_dev, pix), F32)], [pltpu.VMEM((tiles,...  64.5 us
    unnamed x2, local copies, waits for them, and re-layouts  2.69 us

profile of v1, /device:TPU:1, one launch (start us, length us, event | category | flops | bytes accessed | tf_op | source)
XLA Modules:
  0.0 67.8 jit_solution(9587041961676856307)
XLA Ops:
  0.6 64.5 %shard_map.95 = (f32[6,16]{1,0:T(8,128)}, f32[16,768]{1,0:T(8,128)}) custom-call(s32[2,192]{1,0:T(2,128)} %edge_ref.1, f32[3,128]{1,0:T(4,128)} %rot_ref.1, f32[3,128]{1,0:T(4,128)} %trans_ref.1, f32[16,768]{1,0:T(8,128)} %depth_ref.1, f32[16,768]{1,0:T(8,128)} %damp_ref.1, f32[192,2,768]{2,1,0:T(2,128)} %flow_ref.1, f32[192,2,768]{2,1,0:T(2,128)} %weight_ref.1, ...), custom_call_target="tpu_custom_call" | custom-call | tf_op jit(solution)/shard_map/pallas_call | solution.py:726
  65.1 1.3 %copy.12 = f32[6,16]{1,0:T(8,128)} copy(f32[6,16]{1,0:T(8,128)} %get-tuple-element.4) | data formatting | bytes 768
  66.4 1.4 %copy.13 = f32[16,768]{1,0:T(8,128)} copy(f32[16,768]{1,0:T(8,128)} %get-tuple-element.5) | data formatting | bytes 98304

commit v2 on v1

--- a/solution.py
+++ b/solution.py
@@ -1,4 +1,3 @@
-import functools
 import jax
 import jax.numpy as jnp
 from jax import lax
@@ -15,7 +14,6 @@
 BF16 = jnp.bfloat16
 L = 128
 WIN = 32
-SLOT = 24
 BAND = 2 * RADIUS
 PACKED = 160
 VMEM_LIMIT = 60 * 1024 * 1024
@@ -36,7 +34,9 @@
     source = edge_ref[0:1, :] - start + RADIUS
     target = edge_ref[1:2, :] - start + RADIUS
     s = source - RADIUS
-    mine = s * SLOT + target - jnp.where(s >= RADIUS, RADIUS, 0)
+    low = jnp.where(s < f_dev // 2, 1, 0)
+    above = jnp.where(target > source, 1, 0)
+    mine = jnp.where(low == above, 0, f_dev * 8) + s * 8 + (target & 7)
     q = target - RADIUS
     tile = jnp.where(source <= 3, source, jnp.where(source == 7, 4, 6 - source))
     line = jnp.where((source > 3) & (source < 7), q + 7 - source, q)
@@ -67,7 +67,7 @@
 def aggregate(edge_ref, loads, flow3, weight3, mask3, own_ref, low_ref, high_ref, me, f_dev):
     edges = edge_ref.shape[1]
     own = own_ref.shape[1]
-    side = low_ref.shape[1]
+    side = low_ref.shape[2]
     rows = own + 2 * side
     dest = destinations(edge_ref, own, side, f_dev, me)
     pick = (iota((rows, edges), 0) == dest).astype(F32).astype(BF16)
@@ -87,8 +87,8 @@
         for field in range(4):
             part = out[:, field * L : (field + 1) * L]
             own_ref[field, :, cols] = part[:own]
-            low_ref[field, :, cols] = part[own : own + side]
-            high_ref[field, :, cols] = part[own + side :]
+            low_ref[tile, field] = part[own : own + side]
+            high_ref[tile, field] = part[own + side :]
 
 
 def window(load, me, f_dev, frames):
@@ -108,41 +108,98 @@
     return jnp.concatenate([x, jnp.zeros((L - x.shape[0], L), F32)], axis=0).T
 
 
-def jac_sums(u, v, uu, vv, uv, ds, a, b):
+def motion_sums(u, v, uu, vv, a, b, ds):
+    va, ub = v * a, u * b
+    e0, e1 = ds * a, ds * b
+    return [e0, e1, -(u * e0 + v * e1), -(u * va + vv * b), uu * a + v * ub, ub - va]
+
+
+def curvature_sums(u, v, uu, vv, uv, ds, wu, wv):
+    a1, b1 = wu * v, wv * u
+    a2, b2 = a1 * u, b1 * v
+    a3, b3 = wu * uu, wv * vv
+    h00, h11 = wu * ds * ds, wv * ds * ds
+    h02, h12 = h00 * u, h11 * v
+    x1, x2, x3 = ds * a1, ds * a2, ds * a3
+    y1, y2, y3 = ds * b1, ds * b2, ds * b3
     return [
-        ds * a,
-        ds * b,
-        -ds * (u * a + v * b),
-        -uv * a - vv * b,
-        uu * a + uv * b,
-        u * b - v * a,
+        h00, h02, x2, x3, x1,
+        h11, h12, y3, y2, y1,
+        h02 * u + h12 * v, u * x2 + v * y3, u * x3 + v * y2, u * x1 - v * y1,
+        a2 * uv + b3 * vv, a2 * uu + b3 * uv, a2 * v - b3 * u,
+        a3 * uu + b2 * uv, b2 * u - a3 * v,
+        a1 * v + b1 * u,
     ]
 
 
-def adj_t(rel, cor, vec):
-    out = []
-    for j in range(3):
-        out.append(rel[j] * vec[0] + rel[3 + j] * vec[1] + rel[6 + j] * vec[2])
-    for j in range(3):
-        out.append(
-            cor[j] * vec[0]
-            + cor[3 + j] * vec[1]
-            + cor[6 + j] * vec[2]
-            + rel[j] * vec[3]
-            + rel[3 + j] * vec[4]
-            + rel[6 + j] * vec[5]
-        )
-    return out
-
-
-def build(
-    first, pose_ref, own_ref, low_ref, high_ref, depth_ref, damp_ref,
-    matrix_ref, zh_ref, zl_ref, base_ref, scale_ref,
-    frame_ref, pair_ref, hacc, racc, hc, rc, adc, wide, depth3, damp3,
-):
-    f_dev, pix = depth_ref.shape
-    tiles = pix // L
-    half = f_dev // 2
+SIGNS = [1, -1, -1, 1, -1, 1, -1, -1, 1, 1, 1, 1, -1, 1, 1, -1, 1, 1, 1, 1]
+
+
+def adj_t(rel, tr, vec):
+    turn = [
+        vec[3] - (tr[1] * vec[2] - tr[2] * vec[1]),
+        vec[4] - (tr[2] * vec[0] - tr[0] * vec[2]),
+        vec[5] - (tr[0] * vec[1] - tr[1] * vec[0]),
+    ]
+    out = [rel[j] * vec[0] + rel[3 + j] * vec[1] + rel[6 + j] * vec[2] for j in range(3)]
+    return out + [rel[j] * turn[0] + rel[3 + j] * turn[1] + rel[6 + j] * turn[2] for j in range(3)]
+
+
+def fold(x):
+    row = iota((8, L), 0)
+
+    def merge(a, b, bit):
+        other = (row & bit) != 0
+        return jnp.where(other, b, a) + pltpu.roll(jnp.where(other, a, b), bit, 0)
+
+    first, second, third = merge(x[0], x[1], 1), merge(x[2], x[3], 1), merge(x[4], x[5], 1)
+    return merge(merge(first, second, 2), third + pltpu.roll(third, 2, 0), 4)
+
+
+def pair_pose(frame_ref, s, first, after):
+    here = [frame_ref[k, pl.ds(s + RADIUS, 1), :] for k in range(12)]
+    there = [
+        jnp.where(after, frame_ref[k, first : first + 8, :], frame_ref[k, first + 8 : first + 16, :])
+        for k in range(12)
+    ]
+    rel = [
+        there[3 * r] * here[3 * c] + there[3 * r + 1] * here[3 * c + 1] + there[3 * r + 2] * here[3 * c + 2]
+        for r in range(3)
+        for c in range(3)
+    ]
+    tr = [
+        there[9 + r] - (rel[3 * r] * here[9] + rel[3 * r + 1] * here[10] + rel[3 * r + 2] * here[11])
+        for r in range(3)
+    ]
+    return rel, tr
+
+
+def octet(fields, depth, col, rowc, rel, tr):
+    wu, fu, wv, fv = fields
+    point = [
+        rel[3 * k] * col + rel[3 * k + 1] * rowc + rel[3 * k + 2] + depth * tr[k] for k in range(3)
+    ]
+    iz = 1.0 / point[2]
+    u = point[0] * iz
+    v = point[1] * iz
+    ds = depth * iz
+    su = iz * (tr[0] - u * tr[2])
+    sv = iz * (tr[1] - v * tr[2])
+    au = wu * su
+    av = wv * sv
+    gu = wu * (col - u) + fu
+    gv = wv * (rowc - v) + fv
+    uu = 1.0 + u * u
+    vv = 1.0 + v * v
+    uv = u * v
+    e = motion_sums(u, v, uu, vv, au, av, ds)
+    back = fold(adj_t(rel, tr, e))
+    sums = curvature_sums(u, v, uu, vv, uv, ds, wu, wv) + motion_sums(u, v, uu, vv, gu, gv, ds)
+    return e, back, au * su + av * sv, su * gu + sv * gv, sums
+
+
+def prepare(pose_ref, frame_ref, coord_ref, depth_ref, damp_ref, depth3, damp3):
+    tiles = depth3.shape[0]
     ox, oy, oz = pose_ref[0], pose_ref[1], pose_ref[2]
     zero = jnp.zeros_like(ox)
     cross = [[zero, -oz, oy], [oz, zero, -ox], [-oy, ox, zero]]
@@ -154,172 +211,180 @@
             square = cross[r][0] * cross[0][c] + cross[r][1] * cross[1][c] + cross[r][2] * cross[2][c]
             frame_ref[3 * r + c] = float(r == c) + c1 * cross[r][c] + c2 * square
         frame_ref[9 + r] = pose_ref[3 + r]
+    first = lax.axis_index("pix") * (tiles * L)
     for tile in range(tiles):
         depth3[tile] = depth_ref[:, tile * L : (tile + 1) * L]
         damp3[tile] = damp_ref[:, tile * L : (tile + 1) * L]
-    hc[...] = jnp.zeros_like(hc)
-    rc[...] = jnp.zeros_like(rc)
-    adc[...] = jnp.zeros_like(adc)
-    lane = iota((SLOT, L), 1)
-    row = iota((SLOT, L), 0)
-    row8 = iota((8, L), 0)
-
+        pixel = first + tile * L + iota((8, L), 1)
+        prow = pixel // COLS
+        pcol = pixel - prow * COLS
+        coord_ref[tile, 0] = (pcol.astype(F32) - 0.5 * (COLS - 1)) / COLS
+        coord_ref[tile, 1] = (prow.astype(F32) - 0.5 * (ROWS - 1)) / COLS
+
+
+def note(at, sums, pose, sum_ref, pair_ref):
+    for n, x in enumerate(sums):
+        sum_ref[n] = jnp.where(at, jnp.sum(x, axis=1, keepdims=True), sum_ref[n])
+    for n, x in enumerate(pose):
+        pair_ref[n] = jnp.where(at, x, pair_ref[n])
+
+
+def near_pairs(own_ref, frame_ref, coord_ref, depth3, e_ref, part_ref, sum_ref, pair_ref):
+    tiles, f_dev = depth3.shape[:2]
+    half = f_dev // 2
+    row = iota((8, L), 0)
+    lane = iota((8, L), 1)
+    sum_ref[...] = jnp.zeros_like(sum_ref)
+    pair_ref[...] = jnp.zeros_like(pair_ref)
     for part in range(2):
-        base = part * half
-        win = slice(base, base + SLOT)
-        if part == 0:
-            pad = lambda x: jnp.concatenate([x, jnp.zeros((WIN - SLOT, L), F32)], axis=0)
-        else:
-            pad = lambda x: jnp.concatenate([jnp.zeros((WIN - SLOT, L), F32), x], axis=0)
 
         @pl.loop(0, half)
         def per_source(i):
-            s = i + base
-            here = [frame_ref[k, pl.ds(s + RADIUS, 1), :] for k in range(12)]
-            there = [frame_ref[k, win, :] for k in range(12)]
-            rel = [
-                there[3 * r] * here[3 * c]
-                + there[3 * r + 1] * here[3 * c + 1]
-                + there[3 * r + 2] * here[3 * c + 2]
-                for r in range(3)
-                for c in range(3)
-            ]
-            tr = [
-                there[9 + r]
-                - (rel[3 * r] * here[9] + rel[3 * r + 1] * here[10] + rel[3 * r + 2] * here[11])
-                for r in range(3)
-            ]
-            cor = []
-            for c in range(3):
-                cor.append(tr[1] * rel[6 + c] - tr[2] * rel[3 + c])
-            for c in range(3):
-                cor.append(tr[2] * rel[c] - tr[0] * rel[6 + c])
-            for c in range(3):
-                cor.append(tr[0] * rel[3 + c] - tr[1] * rel[c])
-            at = lane == s + RADIUS
-            for k in range(9):
-                pair_ref[k] = rel[k]
-                pair_ref[12 + k] = cor[k]
-                adc[k, win, :] = jnp.where(at, rel[k], adc[k, win, :])
-                adc[9 + k, win, :] = jnp.where(at, cor[k], adc[9 + k, win, :])
-            for k in range(3):
-                pair_ref[9 + k] = tr[k]
-            hacc[...] = jnp.zeros_like(hacc)
-            racc[...] = jnp.zeros_like(racc)
+            s = i + part * half
+            rel, tr = pair_pose(frame_ref, s, 8, row > i if part == 0 else row >= i)
+            sums = None
+            for tile in range(tiles):
+                cols = slice(tile * L, (tile + 1) * L)
+                at = pl.ds(pl.multiple_of(s * 8, 8), 8)
+                fields = [own_ref[k, at, cols] for k in range(4)]
+                e, back, curv, grad, new = octet(
+                    fields, depth3[tile, pl.ds(s, 1), :], coord_ref[tile, 0], coord_ref[tile, 1], rel, tr
+                )
+                slot = s * tiles + tile
+                for j in range(6):
+                    e_ref[slot, j] = e[j]
+                part_ref[slot, 0] = back
+                part_ref[slot, 1] = curv
+                part_ref[slot, 2] = grad
+                sums = new if sums is None else [a + b for a, b in zip(sums, new)]
+            note(lane == s + RADIUS, sums, rel + tr, sum_ref, pair_ref)
+
+
+def far_pairs(
+    own_ref, low_ref, high_ref, frame_ref, coord_ref, depth3, damp3, e_ref, part_ref, sum_ref, pair_ref,
+    base_ref, inv_ref, zs, gram_ref,
+):
+    tiles, f_dev = depth3.shape[:2]
+    half = f_dev // 2
+    row = iota((8, L), 0)
+    lane = iota((8, L), 1)
+    pair = iota((16, L), 0)
+    size = 6 * WIN
+    sum_ref[...] = jnp.zeros_like(sum_ref)
+    pair_ref[...] = jnp.zeros_like(pair_ref)
+    gram_ref[...] = jnp.zeros_like(gram_ref)
+    for ref in zs[2:]:
+        ref[...] = jnp.zeros_like(ref)
+    none = jnp.zeros((8, L), F32)
+
+    def gram(which):
+        zh = zs[2 * which][...]
+        zl = zs[2 * which + 1][...]
+        nt = (((1,), (1,)), ((), ()))
+        gram_ref[0] += lax.dot_general(zh[:size], zh, nt, preferred_element_type=F32)
+        gram_ref[1] += lax.dot_general(zl, zh, nt, preferred_element_type=F32)
+
+    for part in range(2):
+
+        def per_source(i, which):
+            s = i + part * half
+            after = row >= i if part == 0 else row > i
+            rel, tr = pair_pose(frame_ref, s, 0 if part == 0 else 16, after)
             if part == 0:
                 slot = jnp.where(i == 0, 4, jnp.where(i <= 4, i - 1, 7 - i))
                 shift = jnp.where(i > 4, i, 0)
-                keep = row8 >= i
+                keep = row >= i
+                src = high_ref
             else:
                 slot = jnp.where(i <= 3, i, jnp.where(i == 7, 4, 6 - i))
                 shift = jnp.where((i > 3) & (i < 7), i + 1, 0)
-                keep = row8 <= i
-            is_source = row == s + RADIUS - base
-
-            def per_tile(tile):
+                keep = row <= i
+                src = low_ref
+            sums = None
+            for tile in range(tiles):
                 cols = slice(tile * L, (tile + 1) * L)
+                at = pl.ds(pl.multiple_of(f_dev * 8 + s * 8, 8), 8)
                 fields = []
                 for k in range(4):
-                    src = high_ref if part == 0 else low_ref
-                    got = src[k, pl.ds(pl.multiple_of(slot * 8, 8), 8), cols]
-                    got = jnp.where(keep, pltpu.roll(got, shift, 0), 0.0)
-                    if part == 0:
-                        mine = own_ref[k, pl.ds(pl.multiple_of(s * SLOT + 8, 8), 16), cols]
-                        fields.append(jnp.concatenate([got, mine], axis=0))
-                    else:
-                        mine = own_ref[k, pl.ds(pl.multiple_of(s * SLOT, 8), 16), cols]
-                        fields.append(jnp.concatenate([mine, got], axis=0))
-                wu, fu, wv, fv = fields
-                pixel = first + tile * L + iota((1, L), 1)
-                prow = pixel // COLS
-                pcol = pixel - prow * COLS
-                col = (pcol.astype(F32) - 0.5 * (COLS - 1)) / COLS
-                rowc = (prow.astype(F32) - 0.5 * (ROWS - 1)) / COLS
-                depth = depth3[tile, pl.ds(s, 1), :]
-                m = [pair_ref[k] for k in range(21)]
-                point = [
-                    m[3 * k] * col + m[3 * k + 1] * rowc + m[3 * k + 2] + depth * m[9 + k]
-                    for k in range(3)
-                ]
-                iz = 1.0 / point[2]
-                u = point[0] * iz
-                v = point[1] * iz
-                ds = depth * iz
-                su = iz * (m[9] - u * m[11])
-                sv = iz * (m[10] - v * m[11])
-                au = wu * su
-                av = wv * sv
-                gu = wu * (col - u) + fu
-                gv = wv * (rowc - v) + fv
-                curv = jnp.sum(au * su + av * sv, axis=0, keepdims=True) + damp3[tile, pl.ds(s, 1), :]
-                grad = -jnp.sum(su * gu + sv * gv, axis=0, keepdims=True)
-                bstep = grad / curv
+                    got = src[tile, k, pl.ds(pl.multiple_of(slot * 8, 8), 8), :]
+                    fields.append(jnp.where(keep, pltpu.roll(got, shift, 0), own_ref[k, at, cols]))
+                e, back, curv, grad, new = octet(
+                    fields, depth3[tile, pl.ds(s, 1), :], coord_ref[tile, 0], coord_ref[tile, 1], rel, tr
+                )
+                sums = new if sums is None else [a + b for a, b in zip(sums, new)]
+                here = s * tiles + tile
+                for j in range(6):
+                    e_ref[here, 6 + j] = e[j]
+                back = -(back + part_ref[here, 0])
+                e_ref[here, 12] = back
+                curv = jnp.sum(curv + part_ref[here, 1], axis=0, keepdims=True) + damp3[tile, pl.ds(s, 1), :]
+                grad = -jnp.sum(grad + part_ref[here, 2], axis=0, keepdims=True)
+                inv = 1.0 / curv
                 scale = 1.0 / jnp.sqrt(curv)
-                base_ref[tile, pl.ds(s, 1), :] = bstep
-                scale_ref[tile, pl.ds(s, 1), :] = scale
-                uu = 1.0 + u * u
-                vv = 1.0 + v * v
-                uv = u * v
-                e = jac_sums(u, v, uu, vv, uv, ds, au, av)
-                back = adj_t(m[0:9], m[12:21], e)
-                zcols = pl.ds(pl.multiple_of(s * pix + tile * L, L), L)
+                base_ref[tile, pl.ds(s, 1), :] = grad * inv
+                inv_ref[tile, pl.ds(s, 1), :] = inv
+                zh, zl = zs[2 * which], zs[2 * which + 1]
+                source = back * scale
                 for j in range(6):
-                    total = -jnp.sum(back[j], axis=0, keepdims=True)
-                    full = jnp.where(is_source, total, e[j]) * scale
-                    high, low = split(pad(full))
-                    zh_ref[j * WIN : (j + 1) * WIN, zcols] = high
-                    zl_ref[j * WIN : (j + 1) * WIN, zcols] = low
-                r = jac_sums(u, v, uu, vv, uv, ds, -gu - au * bstep, -gv - av * bstep)
-                for j in range(6):
-                    racc[j] += r[j]
-                ju = [ds, None, -ds * u, -uv, uu, -v]
-                jv = [None, ds, -ds * v, -vv, uv, u]
-                wju = [None if x is None else wu * x for x in ju]
-                wjv = [None if x is None else wv * x for x in jv]
-                for n, (a, b) in enumerate(UPPER):
-                    terms = []
-                    if ju[a] is not None and ju[b] is not None:
-                        terms.append(wju[a] * ju[b])
-                    if jv[a] is not None and jv[b] is not None:
-                        terms.append(wjv[a] * jv[b])
-                    hacc[n] += terms[0] if len(terms) == 1 else terms[0] + terms[1]
-
-            for tile in range(tiles):
-                per_tile(tile)
-            for n in range(len(UPPER)):
-                hc[n, win, :] = jnp.where(at, jnp.sum(hacc[n], axis=1, keepdims=True), hc[n, win, :])
-            for j in range(6):
-                rc[j, win, :] = jnp.where(at, jnp.sum(racc[j], axis=1, keepdims=True), rc[j, win, :])
-
-    def accumulate(s, carry):
-        hh, hl = carry
-        cols = pl.ds(pl.multiple_of(s * pix, L), pix)
-        zh = zh_ref[:, cols]
-        zl = zl_ref[:, cols]
-        nt = (((1,), (1,)), ((), ()))
-        return (
-            hh + lax.dot_general(zh, zh, nt, preferred_element_type=F32),
-            hl + lax.dot_general(zh, zl, nt, preferred_element_type=F32),
+                    mine = e[j] * scale
+                    other = e_ref[here, j] * scale
+                    below, over = (mine, other) if part == 0 else (other, mine)
+                    mid = jnp.where(row < i, below, jnp.where(row > i, over, source[j : j + 1, :]))
+                    groups = [jnp.where(row >= i, below, 0.0), mid, jnp.where(row <= i, over, 0.0)]
+                    groups = groups + [none] if part == 0 else [none] + groups
+                    high, low = split(jnp.concatenate(groups, axis=0))
+                    zh[j * WIN : (j + 1) * WIN, cols] = high
+                    zl[j * WIN : (j + 1) * WIN, cols] = low
+                y = grad * scale
+                rest = y - y.astype(BF16).astype(F32)
+                lines = jnp.where(pair == 0, y, jnp.where(pair == 1, rest, 0.0))
+                zh[size : size + 16, cols] = lines.astype(BF16)
+            note(lane == s + RADIUS, sums, rel + tr, sum_ref, pair_ref)
+
+        @pl.loop(0, half // 2)
+        def per_two(k):
+            gram(1)
+            per_source(2 * k, 0)
+            gram(0)
+            per_source(2 * k + 1, 1)
+
+    gram(1)
+
+
+def assemble(near_sum, near_pair, far_sum, far_pair, gram_ref, matrix_ref, wide):
+    size = 6 * WIN
+    row = iota((8, L), 0)
+    lane = iota((8, L), 1)
+    i = lane & 7
+    first = lane < 16
+
+    def sides(near, far):
+        return jnp.where(first, far, near), jnp.where(first, near, far)
+
+    def expand(x):
+        low, high = x
+        mid = jnp.where(row < i, low, jnp.where(row > i, high, 0.0))
+        start = jnp.where(row >= i, low, 0.0)
+        end = jnp.where(row <= i, high, 0.0)
+        return jnp.concatenate(
+            [
+                jnp.where(first, start, 0.0),
+                jnp.where(first, mid, start),
+                jnp.where(first, end, mid),
+                jnp.where(first, 0.0, end),
+            ],
+            axis=0,
         )
 
-    none = jnp.zeros((6 * WIN, 6 * WIN), F32)
-    hh, hl = lax.fori_loop(0, f_dev, accumulate, (none, none))
-
+    pose = [sides(near_pair[k], far_pair[k]) for k in range(12)]
     h = [[None] * 6 for _ in range(6)]
+    wholes = [[None] * 6 for _ in range(6)]
     for n, (a, b) in enumerate(UPPER):
-        h[a][b] = hc[n]
-        h[b][a] = h[a][b]
-    rel = [adc[k] for k in range(9)]
-    cor = [adc[9 + k] for k in range(9)]
-    ad = [[None] * 6 for _ in range(6)]
-    for i in range(3):
-        for j in range(3):
-            ad[i][j] = rel[3 * i + j]
-            ad[i][3 + j] = cor[3 * i + j]
-            ad[3 + i][3 + j] = rel[3 * i + j]
-    lane = iota((WIN, L), 1)
-    row = iota((WIN, L), 0)
-    eye = row == lane
+        pair = sides(near_sum[n], far_sum[n])
+        h[a][b] = h[b][a] = pair if SIGNS[n] > 0 else tuple(-x for x in pair)
+    count = len(UPPER)
+    r = [tuple(-x for x in sides(near_sum[count + j], far_sum[count + j])) for j in range(6)]
+    eye = iota((WIN, L), 0) == iota((WIN, L), 1)
 
     def total(terms):
         out = None
@@ -329,29 +394,58 @@
             out = x * y if out is None else out + x * y
         return out
 
-    had = [[total([(h[i][k], ad[k][j]) for k in range(6)]) for j in range(6)] for i in range(6)]
+    had = [[[None, None] for _ in range(6)] for _ in range(6)]
+    source = [[0.0] * 6 for _ in range(6)]
+    lines = [0.0] * 6
+    for side in range(2):
+        rel = [pose[k][side] for k in range(9)]
+        tr = [pose[9 + k][side] for k in range(3)]
+        ad = [[None] * 6 for _ in range(6)]
+        for c in range(3):
+            corner = [
+                tr[1] * rel[6 + c] - tr[2] * rel[3 + c],
+                tr[2] * rel[c] - tr[0] * rel[6 + c],
+                tr[0] * rel[3 + c] - tr[1] * rel[c],
+            ]
+            for a in range(3):
+                ad[a][c] = ad[3 + a][3 + c] = rel[3 * a + c]
+                ad[a][3 + c] = corner[a]
+        for a in range(6):
+            for b in range(6):
+                had[a][b][side] = total(
+                    [(None if h[a][k] is None else h[a][k][side], ad[k][b]) for k in range(6)]
+                )
+        for a in range(6):
+            for b in range(6):
+                source[a][b] = source[a][b] + total([(ad[k][a], had[k][b][side]) for k in range(6)])
+        back = adj_t(rel, tr, [x[side] for x in r])
+        lines = [x + y for x, y in zip(lines, back)]
     wide[...] = jnp.zeros_like(wide)
     matrix_ref[...] = jnp.zeros_like(matrix_ref)
-    for i in range(6):
-        rows = slice(i * WIN, (i + 1) * WIN)
-        for j in range(6):
-            cols = slice(j * WIN, (j + 1) * WIN)
-            wide[rows, cols] = -had[i][j][:, :WIN]
-            both = jnp.sum(total([(ad[k][i], had[k][j]) for k in range(6)]), axis=0, keepdims=True)
-            if h[i][j] is not None:
-                both = both + jnp.sum(h[i][j], axis=1, keepdims=True)
-            diag = jnp.where(eye, both, 0.0)
-            matrix_ref[rows, cols] = diag[:, :WIN]
-    wide[: 6 * WIN, : 6 * WIN] = wide[: 6 * WIN, : 6 * WIN] - hl
+    for a in range(6):
+        rows = slice(a * WIN, (a + 1) * WIN)
+        for b in range(6):
+            cols = slice(b * WIN, (b + 1) * WIN)
+            wide[rows, cols] = -expand(had[a][b])[:, :WIN]
+            both = jnp.sum(source[a][b], axis=0, keepdims=True)
+            if h[a][b] is not None:
+                both = both + jnp.sum(expand(h[a][b]), axis=1, keepdims=True)
+            matrix_ref[rows, cols] = jnp.where(eye, both, 0.0)[:, :WIN]
+    high, low = gram_ref[0], gram_ref[1]
+    wide[:size, :size] = wide[:size, :size] - low[:, :size]
+    wide[:size, size : size + 1] = -(
+        high[:, size : size + 1] + high[:, size + 1 : size + 2] + low[:, size : size + 1]
+    )
     flipped = wide[...].T
-    matrix_ref[: 6 * WIN, : 6 * WIN] = (
-        matrix_ref[: 6 * WIN, : 6 * WIN] - hh + wide[: 6 * WIN, : 6 * WIN] + flipped[: 6 * WIN, : 6 * WIN]
+    matrix_ref[:size, :size] = (
+        matrix_ref[:size, :size] - high[:, :size] + wide[:size, :size] + flipped[:size, :size]
     )
-    r = [rc[j] for j in range(6)]
-    back = adj_t(rel, cor, r)
     for j in range(6):
-        here = jnp.sum(jnp.where(eye, jnp.sum(r[j], axis=1, keepdims=True), 0.0) - back[j], axis=0, keepdims=True)
-        matrix_ref[6 * WIN : 6 * WIN + 1, j * WIN : (j + 1) * WIN] = here[:, :WIN]
+        cols = slice(j * WIN, (j + 1) * WIN)
+        whole = jnp.sum(expand(r[j]), axis=1, keepdims=True)
+        here = jnp.sum(jnp.where(eye, whole, 0.0), axis=0, keepdims=True)
+        here = here - jnp.sum(lines[j], axis=0, keepdims=True)
+        matrix_ref[size : size + 1, cols] = here[:, :WIN] + flipped[size : size + 1, cols]
 
 
 def remote(src, dst, sems, phase, which, axis, peer):
@@ -586,12 +680,13 @@
 
 
 def finish(
-    matrix_ref, zh_ref, zl_ref, base_ref, scale_ref, pose_ref, step_ref, frames,
+    matrix_ref, e_ref, base_ref, inv_ref, pose_ref, step_ref, frames,
     cols_ref, step3, packed_ref, land, reduced_ref, gathered, diag_ref, ahead_ref, back_ref, far_ref, x_ref,
     pix_sem, round_sem,
 ):
     me = lax.axis_index("frames")
-    f_dev, pix = step_ref.shape
+    tiles, f_dev = step3.shape[:2]
+    half = f_dev // 2
     pack(matrix_ref, packed_ref)
     rhs, later = operator(
         packed_ref, land, reduced_ref, gathered, diag_ref, ahead_ref, back_ref, far_ref,
@@ -604,39 +699,57 @@
     pose_ref[...] = mine[:6, RADIUS : RADIUS + f_dev]
     turned = spread_rows(mine)
     for i in range(6):
-        cols_ref[i * WIN : (i + 1) * WIN, :] = jnp.broadcast_to(turned[:WIN, i : i + 1], (WIN, L))
-
-    @pl.loop(0, f_dev)
-    def per_source(s):
-        for tile in range(pix // L):
-            zcols = pl.ds(pl.multiple_of(s * pix + tile * L, L), L)
-            z = zh_ref[:, zcols].astype(F32) + zl_ref[:, zcols].astype(F32)
-            image = jnp.sum(z * cols_ref[...], axis=0, keepdims=True)
-            here = (tile, pl.ds(s, 1), slice(None))
-            step3[here] = base_ref[here] - scale_ref[here] * image
-
-    for tile in range(pix // L):
+        cols_ref[i] = jnp.broadcast_to(turned[:WIN, i : i + 1], (WIN, L))
+    row = iota((8, L), 0)
+    lane = iota((8, L), 1)
+    for part in range(2):
+
+        @pl.loop(0, half)
+        def per_source(i):
+            s = i + part * half
+            group = [[cols_ref[j, 8 * g : 8 * g + 8, :] for g in range(part, part + 3)] for j in range(6)]
+            below = [jnp.where(row >= i, group[j][0], group[j][1]) for j in range(6)]
+            over = [jnp.where(row > i, group[j][1], group[j][2]) for j in range(6)]
+            near, far = (over, below) if part == 0 else (below, over)
+            at = jnp.sum(jnp.where(lane == s + RADIUS, mine, 0.0), axis=1, keepdims=True)
+            terms = near + far + [jnp.broadcast_to(at, (8, L))]
+            for tile in range(tiles):
+                slot = s * tiles + tile
+                image = e_ref[slot, 0] * terms[0]
+                for n in range(1, 13):
+                    image = image + e_ref[slot, n] * terms[n]
+                image = jnp.sum(image, axis=0, keepdims=True)
+                here = (tile, pl.ds(s, 1), slice(None))
+                step3[here] = base_ref[here] - inv_ref[here] * image
+
+    for tile in range(tiles):
         step_ref[:, tile * L : (tile + 1) * L] = step3[tile]
 
 
 def swap_edges(low_out, high_out, low_ref, high_ref, sems):
     count = lax.axis_size("frames")
     me = lax.axis_index("frames")
-    down = remote(low_out, low_ref, sems, 0, 0, "frames", lax.rem(me + count - 1, count))
-    up = remote(high_out, high_ref, sems, 1, 0, "frames", lax.rem(me + 1, count))
+    below = lax.rem(me + count - 1, count)
+    over = lax.rem(me + 1, count)
+    tiles = low_out.shape[0]
+    down = [remote(low_out.at[t], low_ref.at[t], sems, 0, t, "frames", below) for t in range(tiles)]
+    up = [remote(high_out.at[t], high_ref.at[t], sems, 1, t, "frames", over) for t in range(tiles)]
 
     @pl.when(me > 0)
     def _():
-        down.start()
+        for copy in down:
+            copy.start()
 
     @pl.when(me < count - 1)
     def _():
-        up.start()
+        for copy in up:
+            copy.start()
 
     def receive():
         @pl.when(me < count - 1)
         def _():
-            down.wait_recv()
+            for copy in down:
+                copy.wait_recv()
 
         @pl.when(me == count - 1)
         def _():
@@ -644,7 +757,8 @@
 
         @pl.when(me > 0)
         def _():
-            up.wait_recv()
+            for copy in up:
+                copy.wait_recv()
 
         @pl.when(me == 0)
         def _():
@@ -653,11 +767,13 @@
     def drain():
         @pl.when(me > 0)
         def _():
-            down.wait_send()
+            for copy in down:
+                copy.wait_send()
 
         @pl.when(me < count - 1)
         def _():
-            up.wait_send()
+            for copy in up:
+                copy.wait_send()
 
     return receive, drain
 
@@ -665,9 +781,10 @@
 def solve(
     edge_ref, rot_ref, trans_ref, depth_ref, damp_ref, flow_ref, weight_ref, mask_ref,
     x_ref, step_ref, flow3, weight3, mask3, load_sem, pose_ref,
-    own_ref, low_out, high_out, low_ref, high_ref, edge_sem, *scratch,
+    own_ref, low_out, high_out, low_ref, high_ref, edge_sem,
+    frame_ref, coord_ref, depth3, damp3, e_ref, part_ref, near_sum, near_pair, far_sum, far_pair,
+    base_ref, inv_ref, zh0, zl0, zh1, zl1, gram_ref, matrix_ref, wide, *scratch,
 ):
-    matrix, zh, zl, base, scale = scratch[:5]
     me = lax.axis_index("frames")
     f_dev, pix = depth_ref.shape
     frames = rot_ref.shape[1]
@@ -686,16 +803,19 @@
     turned = spread_rows(jnp.concatenate(poses, axis=0))
     for k in range(6):
         pose_ref[k] = jnp.broadcast_to(turned[:WIN, k : k + 1], (WIN, L))
+    prepare(pose_ref, frame_ref, coord_ref, depth_ref, damp_ref, depth3, damp3)
     aggregate(edge_ref, loads, flow3, weight3, mask3, own_ref, low_out, high_out, me, f_dev)
     pl.semaphore_wait(barrier, total)
     receive, drain = swap_edges(low_out, high_out, low_ref, high_ref, edge_sem)
+    near_pairs(own_ref, frame_ref, coord_ref, depth3, e_ref, part_ref, near_sum, near_pair)
     receive()
+    far_pairs(
+        own_ref, low_ref, high_ref, frame_ref, coord_ref, depth3, damp3, e_ref, part_ref,
+        far_sum, far_pair, base_ref, inv_ref, (zh0, zl0, zh1, zl1), gram_ref,
+    )
+    assemble(near_sum, near_pair, far_sum, far_pair, gram_ref, matrix_ref, wide)
+    finish(matrix_ref, e_ref, base_ref, inv_ref, x_ref, step_ref, frames, *scratch)
     drain()
-    build(
-        lax.axis_index("pix") * pix, pose_ref, own_ref, low_ref, high_ref, depth_ref, damp_ref,
-        matrix, zh, zl, base, scale, *scratch[5:15],
-    )
-    finish(matrix, zh, zl, base, scale, x_ref, step_ref, frames, *scratch[15:])
 
 
 def call(body, out, scratch, vmem, hbm, **params):
@@ -716,10 +836,11 @@
     edges = mask.shape[0]
     frames = rotvec.shape[1]
     tiles = pix // L
-    own_rows = f_dev * SLOT
+    own_rows = f_dev * 16
     side = 40
-    n = len(UPPER)
+    sums = len(UPPER) + 6
     width = 256
+    size = 6 * WIN
     count = lax.axis_size("frames")
     zcount = lax.axis_size("pix")
     chunk = -(-PACKED // (8 * zcount)) * 8
@@ -733,27 +854,31 @@
             pltpu.SemaphoreType.DMA((tiles, 5)),
             pltpu.VMEM((6, WIN, L), F32),
             pltpu.VMEM((4, own_rows, pix), F32),
-            pltpu.VMEM((4, side, pix), F32),
-            pltpu.VMEM((4, side, pix), F32),
-            pltpu.VMEM((4, side, pix), F32),
-            pltpu.VMEM((4, side, pix), F32),
-            pltpu.SemaphoreType.DMA((2, 2, 1)),
-            pltpu.VMEM((6 * WIN + 8, width), F32),
-            pltpu.VMEM((6 * WIN, f_dev * pix), BF16),
-            pltpu.VMEM((6 * WIN, f_dev * pix), BF16),
+            pltpu.VMEM((tiles, 4, side, L), F32),
+            pltpu.VMEM((tiles, 4, side, L), F32),
+            pltpu.VMEM((tiles, 4, side, L), F32),
+            pltpu.VMEM((tiles, 4, side, L), F32),
+            pltpu.SemaphoreType.DMA((2, 2, tiles)),
+            pltpu.VMEM((12, WIN, L), F32),
+            pltpu.VMEM((tiles, 2, 8, L), F32),
             pltpu.VMEM((tiles, f_dev, L), F32),
             pltpu.VMEM((tiles, f_dev, L), F32),
-            pltpu.VMEM((12, WIN, L), F32),
-            pltpu.VMEM((21, SLOT, L), F32),
-            pltpu.VMEM((n, SLOT, L), F32),
-            pltpu.VMEM((6, SLOT, L), F32),
-            pltpu.VMEM((n, WIN, L), F32),
-            pltpu.VMEM((6, WIN, L), F32),
-            pltpu.VMEM((18, WIN, L), F32),
-            pltpu.VMEM((256, 256), F32),
+            pltpu.VMEM((f_dev * tiles, 13, 8, L), F32),
+            pltpu.VMEM((f_dev * tiles, 3, 8, L), F32),
+            pltpu.VMEM((sums, 8, L), F32),
+            pltpu.VMEM((12, 8, L), F32),
+            pltpu.VMEM((sums, 8, L), F32),
+            pltpu.VMEM((12, 8, L), F32),
             pltpu.VMEM((tiles, f_dev, L), F32),
             pltpu.VMEM((tiles, f_dev, L), F32),
-            pltpu.VMEM((6 * WIN, L), F32),
+            pltpu.VMEM((size + 16, pix), BF16),
+            pltpu.VMEM((size, pix), BF16),
+            pltpu.VMEM((size + 16, pix), BF16),
+            pltpu.VMEM((size, pix), BF16),
+            pltpu.VMEM((2, size, size + 16), F32),
+            pltpu.VMEM((size + 8, width), F32),
+            pltpu.VMEM((256, 256), F32),
+            pltpu.VMEM((6, WIN, L), F32),
             pltpu.VMEM((tiles, f_dev, L), F32),
             pltpu.VMEM((chunk * zcount, L), F32),
             pltpu.VMEM((zcount, chunk, L), F32),

time: 68.6 us -> 52.8 us (0.77)
  Pallas kernels: 64.5 us -> 48.7 us
    pallas_call x1, Pallas kernels: 64.5 us -> 48.7 us  [per_device(): call(solve, [((6, f_dev), F32), ((f_dev, pix), F32)], [pltpu.VMEM((tiles,...]
where the time goes in v2:
time: 52.8 us; the launch traced here: 52 us
  Pallas kernels  48.7 us (92%)
  local copies, waits for them, and re-layouts  2.69 us (5%)
  between operations  0.64 us (1%)
    pallas_call x1, Pallas kernels, per_device(): call(solve, [((6, f_dev), F32), ((f_dev, pix), F32)], [pltpu.VMEM((tiles,...  48.7 us
    unnamed x2, local copies, waits for them, and re-layouts  2.69 us

profile of v2, /device:TPU:1, one launch (start us, length us, event | category | flops | bytes accessed | tf_op | source)
XLA Modules:
  0.0 52.0 jit_solution(9645573891124345937)
XLA Ops:
  0.6 48.7 %shard_map.95 = (f32[6,16]{1,0:T(8,128)}, f32[16,768]{1,0:T(8,128)}) custom-call(s32[2,192]{1,0:T(2,128)} %edge_ref.1, f32[3,128]{1,0:T(4,128)} %rot_ref.1, f32[3,128]{1,0:T(4,128)} %trans_ref.1, f32[16,768]{1,0:T(8,128)} %depth_ref.1, f32[16,768]{1,0:T(8,128)} %damp_ref.1, f32[192,2,768]{2,1,0:T(2,128)} %flow_ref.1, f32[192,2,768]{2,1,0:T(2,128)} %weight_ref.1, ...), custom_call_target="tpu_custom_call" | custom-call | tf_op jit(solution)/shard_map/pallas_call | solution.py:847
  49.3 1.3 %copy.12 = f32[6,16]{1,0:T(8,128)} copy(f32[6,16]{1,0:T(8,128)} %get-tuple-element.4) | data formatting | bytes 768
  50.6 1.4 %copy.13 = f32[16,768]{1,0:T(8,128)} copy(f32[16,768]{1,0:T(8,128)} %get-tuple-element.5) | data formatting | bytes 98304

commit v3 on v2

--- a/solution.py
+++ b/solution.py
@@ -16,6 +16,7 @@
 WIN = 32
 BAND = 2 * RADIUS
 PACKED = 160
+SENT = RADIUS * (RADIUS + 1) // 2
 VMEM_LIMIT = 60 * 1024 * 1024
 UPPER = [(i, j) for i in range(6) for j in range(i, 6) if (i, j) != (0, 1)]
 
@@ -38,13 +39,13 @@
     above = jnp.where(target > source, 1, 0)
     mine = jnp.where(low == above, 0, f_dev * 8) + s * 8 + (target & 7)
     q = target - RADIUS
-    tile = jnp.where(source <= 3, source, jnp.where(source == 7, 4, 6 - source))
+    tile = jnp.where(source < 3, source, jnp.where(source == 3, 4, jnp.where(source == 7, 3, 6 - source)))
     line = jnp.where((source > 3) & (source < 7), q + 7 - source, q)
     lowest = own_rows + tile * 8 + line
     i = source - f_dev - RADIUS
     q = target - f_dev
-    tile = jnp.where(i == 0, 4, jnp.where(i <= 4, i - 1, 7 - i))
-    line = jnp.where(i > 4, q - i, q)
+    tile = jnp.where(i == 0, 3, jnp.where(i < 4, i - 1, jnp.where(i == 4, 4, 7 - i)))
+    line = jnp.where(i >= 4, q - i, q)
     highest = own_rows + side + tile * 8 + line
     return jnp.where(source < RADIUS, lowest, jnp.where(source >= RADIUS + f_dev, highest, mine))
 
@@ -229,7 +230,7 @@
         pair_ref[n] = jnp.where(at, x, pair_ref[n])
 
 
-def near_pairs(own_ref, frame_ref, coord_ref, depth3, e_ref, part_ref, sum_ref, pair_ref):
+def near_pairs(own_ref, frame_ref, coord_ref, depth3, e_ref, part_ref, sum_ref, pair_ref, descend):
     tiles, f_dev = depth3.shape[:2]
     half = f_dev // 2
     row = iota((8, L), 0)
@@ -259,10 +260,13 @@
                 sums = new if sums is None else [a + b for a, b in zip(sums, new)]
             note(lane == s + RADIUS, sums, rel + tr, sum_ref, pair_ref)
 
+        if part == 1:
+            descend()
+
 
 def far_pairs(
     own_ref, low_ref, high_ref, frame_ref, coord_ref, depth3, damp3, e_ref, part_ref, sum_ref, pair_ref,
-    base_ref, inv_ref, zs, gram_ref,
+    base_ref, inv_ref, zs, gram_ref, receive,
 ):
     tiles, f_dev = depth3.shape[:2]
     half = f_dev // 2
@@ -285,18 +289,19 @@
         gram_ref[1] += lax.dot_general(zl, zh, nt, preferred_element_type=F32)
 
     for part in range(2):
+        receive(part)
 
         def per_source(i, which):
             s = i + part * half
             after = row >= i if part == 0 else row > i
             rel, tr = pair_pose(frame_ref, s, 0 if part == 0 else 16, after)
             if part == 0:
-                slot = jnp.where(i == 0, 4, jnp.where(i <= 4, i - 1, 7 - i))
-                shift = jnp.where(i > 4, i, 0)
+                slot = jnp.where(i == 0, 3, jnp.where(i < 4, i - 1, jnp.where(i == 4, 4, 7 - i)))
+                shift = jnp.where(i >= 4, i, 0)
                 keep = row >= i
                 src = high_ref
             else:
-                slot = jnp.where(i <= 3, i, jnp.where(i == 7, 4, 6 - i))
+                slot = jnp.where(i < 3, i, jnp.where(i == 3, 4, jnp.where(i == 7, 3, 6 - i)))
                 shift = jnp.where((i > 3) & (i < 7), i + 1, 0)
                 keep = row <= i
                 src = low_ref
@@ -732,37 +737,42 @@
     below = lax.rem(me + count - 1, count)
     over = lax.rem(me + 1, count)
     tiles = low_out.shape[0]
-    down = [remote(low_out.at[t], low_ref.at[t], sems, 0, t, "frames", below) for t in range(tiles)]
-    up = [remote(high_out.at[t], high_ref.at[t], sems, 1, t, "frames", over) for t in range(tiles)]
-
-    @pl.when(me > 0)
-    def _():
-        for copy in down:
-            copy.start()
+    down = [remote(low_out.at[t, :, :SENT], low_ref.at[t, :, :SENT], sems, 0, t, "frames", below) for t in range(tiles)]
+    up = [remote(high_out.at[t, :, :SENT], high_ref.at[t, :, :SENT], sems, 1, t, "frames", over) for t in range(tiles)]
 
     @pl.when(me < count - 1)
     def _():
         for copy in up:
             copy.start()
 
-    def receive():
-        @pl.when(me < count - 1)
+    def descend():
+        @pl.when(me > 0)
         def _():
             for copy in down:
-                copy.wait_recv()
-
-        @pl.when(me == count - 1)
-        def _():
-            low_ref[...] = jnp.zeros_like(low_ref)
-
-        @pl.when(me > 0)
-        def _():
-            for copy in up:
-                copy.wait_recv()
-
-        @pl.when(me == 0)
-        def _():
-            high_ref[...] = jnp.zeros_like(high_ref)
+                copy.start()
+
+    def receive(part):
+        if part == 0:
+
+            @pl.when(me > 0)
+            def _():
+                for copy in up:
+                    copy.wait_recv()
+
+            @pl.when(me == 0)
+            def _():
+                high_ref[...] = jnp.zeros_like(high_ref)
+
+        else:
+
+            @pl.when(me < count - 1)
+            def _():
+                for copy in down:
+                    copy.wait_recv()
+
+            @pl.when(me == count - 1)
+            def _():
+                low_ref[...] = jnp.zeros_like(low_ref)
 
     def drain():
         @pl.when(me > 0)
@@ -775,7 +785,7 @@
             for copy in up:
                 copy.wait_send()
 
-    return receive, drain
+    return descend, receive, drain
 
 
 def solve(
@@ -806,12 +816,11 @@
     prepare(pose_ref, frame_ref, coord_ref, depth_ref, damp_ref, depth3, damp3)
     aggregate(edge_ref, loads, flow3, weight3, mask3, own_ref, low_out, high_out, me, f_dev)
     pl.semaphore_wait(barrier, total)
-    receive, drain = swap_edges(low_out, high_out, low_ref, high_ref, edge_sem)
-    near_pairs(own_ref, frame_ref, coord_ref, depth3, e_ref, part_ref, near_sum, near_pair)
-    receive()
+    descend, receive, drain = swap_edges(low_out, high_out, low_ref, high_ref, edge_sem)
+    near_pairs(own_ref, frame_ref, coord_ref, depth3, e_ref, part_ref, near_sum, near_pair, descend)
     far_pairs(
         own_ref, low_ref, high_ref, frame_ref, coord_ref, depth3, damp3, e_ref, part_ref,
-        far_sum, far_pair, base_ref, inv_ref, (zh0, zl0, zh1, zl1), gram_ref,
+        far_sum, far_pair, base_ref, inv_ref, (zh0, zl0, zh1, zl1), gram_ref, receive,
     )
     assemble(near_sum, near_pair, far_sum, far_pair, gram_ref, matrix_ref, wide)
     finish(matrix_ref, e_ref, base_ref, inv_ref, x_ref, step_ref, frames, *scratch)

time: 52.8 us -> 48.3 us (0.915)
  Pallas kernels: 48.7 us -> 44.1 us
    pallas_call x1, Pallas kernels: 48.7 us -> 44.1 us  [per_device(): call(solve, [((6, f_dev), F32), ((f_dev, pix), F32)], [pltpu.VMEM((tiles,...]
where the time goes in v3:
time: 48.3 us; the launch traced here: 47.4 us
  Pallas kernels  44.1 us (91%)
  local copies, waits for them, and re-layouts  2.69 us (6%)
  between operations  0.64 us (1%)
    pallas_call x1, Pallas kernels, per_device(): call(solve, [((6, f_dev), F32), ((f_dev, pix), F32)], [pltpu.VMEM((tiles,...  44.1 us
    unnamed x2, local copies, waits for them, and re-layouts  2.69 us

profile of v3, /device:TPU:1, one launch (start us, length us, event | category | flops | bytes accessed | tf_op | source)
XLA Modules:
  0.0 47.4 jit_solution(14386391254064257581)
XLA Ops:
  0.6 44.1 %shard_map.95 = (f32[6,16]{1,0:T(8,128)}, f32[16,768]{1,0:T(8,128)}) custom-call(s32[2,192]{1,0:T(2,128)} %edge_ref.1, f32[3,128]{1,0:T(4,128)} %rot_ref.1, f32[3,128]{1,0:T(4,128)} %trans_ref.1, f32[16,768]{1,0:T(8,128)} %depth_ref.1, f32[16,768]{1,0:T(8,128)} %damp_ref.1, f32[192,2,768]{2,1,0:T(2,128)} %flow_ref.1, f32[192,2,768]{2,1,0:T(2,128)} %weight_ref.1, ...), custom_call_target="tpu_custom_call" | custom-call | tf_op jit(solution)/shard_map/pallas_call | solution.py:856
  44.7 1.3 %copy.12 = f32[6,16]{1,0:T(8,128)} copy(f32[6,16]{1,0:T(8,128)} %get-tuple-element.4) | data formatting | bytes 768
  46.0 1.4 %copy.13 = f32[16,768]{1,0:T(8,128)} copy(f32[16,768]{1,0:T(8,128)} %get-tuple-element.5) | data formatting | bytes 98304

commit v4 on v3

--- a/solution.py
+++ b/solution.py
@@ -277,16 +277,13 @@
     sum_ref[...] = jnp.zeros_like(sum_ref)
     pair_ref[...] = jnp.zeros_like(pair_ref)
     gram_ref[...] = jnp.zeros_like(gram_ref)
-    for ref in zs[2:]:
-        ref[...] = jnp.zeros_like(ref)
+    zs[1][...] = jnp.zeros_like(zs[1])
     none = jnp.zeros((8, L), F32)
 
     def gram(which):
-        zh = zs[2 * which][...]
-        zl = zs[2 * which + 1][...]
+        z = zs[which][...]
         nt = (((1,), (1,)), ((), ()))
-        gram_ref[0] += lax.dot_general(zh[:size], zh, nt, preferred_element_type=F32)
-        gram_ref[1] += lax.dot_general(zl, zh, nt, preferred_element_type=F32)
+        gram_ref[...] += lax.dot_general(z, z[: size + 16], nt, preferred_element_type=F32)
 
     for part in range(2):
         receive(part)
@@ -328,7 +325,8 @@
                 scale = 1.0 / jnp.sqrt(curv)
                 base_ref[tile, pl.ds(s, 1), :] = grad * inv
                 inv_ref[tile, pl.ds(s, 1), :] = inv
-                zh, zl = zs[2 * which], zs[2 * which + 1]
+                z = zs[which]
+                skip = size + 16
                 source = back * scale
                 for j in range(6):
                     mine = e[j] * scale
@@ -338,12 +336,12 @@
                     groups = [jnp.where(row >= i, below, 0.0), mid, jnp.where(row <= i, over, 0.0)]
                     groups = groups + [none] if part == 0 else [none] + groups
                     high, low = split(jnp.concatenate(groups, axis=0))
-                    zh[j * WIN : (j + 1) * WIN, cols] = high
-                    zl[j * WIN : (j + 1) * WIN, cols] = low
+                    z[j * WIN : (j + 1) * WIN, cols] = high
+                    z[skip + j * WIN : skip + (j + 1) * WIN, cols] = low
                 y = grad * scale
                 rest = y - y.astype(BF16).astype(F32)
                 lines = jnp.where(pair == 0, y, jnp.where(pair == 1, rest, 0.0))
-                zh[size : size + 16, cols] = lines.astype(BF16)
+                z[size : size + 16, cols] = lines.astype(BF16)
             note(lane == s + RADIUS, sums, rel + tr, sum_ref, pair_ref)
 
         @pl.loop(0, half // 2)
@@ -436,7 +434,7 @@
             if h[a][b] is not None:
                 both = both + jnp.sum(expand(h[a][b]), axis=1, keepdims=True)
             matrix_ref[rows, cols] = jnp.where(eye, both, 0.0)[:, :WIN]
-    high, low = gram_ref[0], gram_ref[1]
+    high, low = gram_ref[:size, :], gram_ref[size + 16 :, :]
     wide[:size, :size] = wide[:size, :size] - low[:, :size]
     wide[:size, size : size + 1] = -(
         high[:, size : size + 1] + high[:, size + 1 : size + 2] + low[:, size : size + 1]
@@ -512,7 +510,7 @@
     return sent
 
 
-def operator(packed_ref, land, reduced_ref, gathered, diag_ref, ahead_ref, back_ref, far_ref, pix_sem, round_sem, f_dev, frames):
+def operator(packed_ref, land, reduced_ref, gathered, diag_ref, ahead_ref, back_ref, far_ref, pix_sem, round_sem, mate_sem, f_dev, frames):
     zcount = lax.axis_size("pix")
     z = lax.axis_index("pix")
     count = lax.axis_size("frames")
@@ -553,10 +551,20 @@
             diag_ref[z, k, :, tile * L : (tile + 1) * L] = sums[k][tile]
     for copy in sent + more:
         copy.wait_send()
-    sent = exchange(lambda peer: diag_ref.at[z], diag_ref.at[z], pix_sem, 1, "pix")
-    for copy in sent:
+    mate = me + 1 - 2 * lax.rem(me, 2)
+    mine = pl.ds(2 * lax.rem(me, 2), 2)
+    half = diag_ref.at[z, mine]
+    sent = exchange(lambda peer: half, half, pix_sem, 1, "pix")
+    passed = []
+    for n, (copy, step) in enumerate(zip(sent, range(zcount - 1, 0, -1))):
         copy.wait_recv()
-    for copy in sent:
+        there = diag_ref.at[lax.rem(z + step, zcount), mine]
+        handed = remote(there, there, mate_sem, 0, n, "frames", mate)
+        handed.start()
+        passed.append(handed)
+    for copy in passed:
+        copy.wait_recv()
+    for copy in sent + passed:
         copy.wait_send()
 
     def block(k, at):
@@ -687,7 +695,7 @@
 def finish(
     matrix_ref, e_ref, base_ref, inv_ref, pose_ref, step_ref, frames,
     cols_ref, step3, packed_ref, land, reduced_ref, gathered, diag_ref, ahead_ref, back_ref, far_ref, x_ref,
-    pix_sem, round_sem,
+    pix_sem, round_sem, mate_sem,
 ):
     me = lax.axis_index("frames")
     tiles, f_dev = step3.shape[:2]
@@ -695,7 +703,7 @@
     pack(matrix_ref, packed_ref)
     rhs, later = operator(
         packed_ref, land, reduced_ref, gathered, diag_ref, ahead_ref, back_ref, far_ref,
-        pix_sem, round_sem, f_dev, frames,
+        pix_sem, round_sem, mate_sem, f_dev, frames,
     )
     x = conjugate(rhs, later, ahead_ref, back_ref, far_ref)
     for t, value in enumerate(x):
@@ -793,7 +801,7 @@
     x_ref, step_ref, flow3, weight3, mask3, load_sem, pose_ref,
     own_ref, low_out, high_out, low_ref, high_ref, edge_sem,
     frame_ref, coord_ref, depth3, damp3, e_ref, part_ref, near_sum, near_pair, far_sum, far_pair,
-    base_ref, inv_ref, zh0, zl0, zh1, zl1, gram_ref, matrix_ref, wide, *scratch,
+    base_ref, inv_ref, z0, z1, gram_ref, matrix_ref, wide, *scratch,
 ):
     me = lax.axis_index("frames")
     f_dev, pix = depth_ref.shape
@@ -820,7 +828,7 @@
     near_pairs(own_ref, frame_ref, coord_ref, depth3, e_ref, part_ref, near_sum, near_pair, descend)
     far_pairs(
         own_ref, low_ref, high_ref, frame_ref, coord_ref, depth3, damp3, e_ref, part_ref,
-        far_sum, far_pair, base_ref, inv_ref, (zh0, zl0, zh1, zl1), gram_ref, receive,
+        far_sum, far_pair, base_ref, inv_ref, (z0, z1), gram_ref, receive,
     )
     assemble(near_sum, near_pair, far_sum, far_pair, gram_ref, matrix_ref, wide)
     finish(matrix_ref, e_ref, base_ref, inv_ref, x_ref, step_ref, frames, *scratch)
@@ -880,11 +888,9 @@
             pltpu.VMEM((12, 8, L), F32),
             pltpu.VMEM((tiles, f_dev, L), F32),
             pltpu.VMEM((tiles, f_dev, L), F32),
-            pltpu.VMEM((size + 16, pix), BF16),
-            pltpu.VMEM((size, pix), BF16),
-            pltpu.VMEM((size + 16, pix), BF16),
-            pltpu.VMEM((size, pix), BF16),
-            pltpu.VMEM((2, size, size + 16), F32),
+            pltpu.VMEM((2 * size + 16, pix), BF16),
+            pltpu.VMEM((2 * size + 16, pix), BF16),
+            pltpu.VMEM((2 * size + 16, size + 16), F32),
             pltpu.VMEM((size + 8, width), F32),
             pltpu.VMEM((256, 256), F32),
             pltpu.VMEM((6, WIN, L), F32),
@@ -900,6 +906,7 @@
             pltpu.VMEM((8, frames), F32),
             pltpu.SemaphoreType.DMA((2, 2, zcount)),
             pltpu.SemaphoreType.DMA((2, 1, count)),
+            pltpu.SemaphoreType.DMA((2, 1, zcount)),
         ],
         5, 3, collective_id=0, has_side_effects=True,
     )(edge_frames, rotvec, trans, inv_depth, depth_damping, flow, weight, mask)

time: 48.3 us -> 46 us (0.952); the launches traced: 47.4 us -> 45.6 us
  Pallas kernels: 44.1 us -> 42.3 us
    pallas_call x1, Pallas kernels: 44.1 us -> 42.3 us  [per_device(): call(solve, [((6, f_dev), F32), ((f_dev, pix), F32)], [pltpu.VMEM((tiles,...]
where the time goes in v4:
time: 46 us; the launch traced here: 45.6 us
  Pallas kernels  42.3 us (92%)
  local copies, waits for them, and re-layouts  2.69 us (6%)
  between operations  0.64 us (1%)
    pallas_call x1, Pallas kernels, per_device(): call(solve, [((6, f_dev), F32), ((f_dev, pix), F32)], [pltpu.VMEM((tiles,...  42.3 us
    unnamed x2, local copies, waits for them, and re-layouts  2.69 us

profile of v4, /device:TPU:1, one launch (start us, length us, event | category | flops | bytes accessed | tf_op | source)
XLA Modules:
  0.0 45.6 jit_solution(10549517218707912777)
XLA Ops:
  0.6 42.3 %shard_map.95 = (f32[6,16]{1,0:T(8,128)}, f32[16,768]{1,0:T(8,128)}) custom-call(s32[2,192]{1,0:T(2,128)} %edge_ref.1, f32[3,128]{1,0:T(4,128)} %rot_ref.1, f32[3,128]{1,0:T(4,128)} %trans_ref.1, f32[16,768]{1,0:T(8,128)} %depth_ref.1, f32[16,768]{1,0:T(8,128)} %damp_ref.1, f32[192,2,768]{2,1,0:T(2,128)} %flow_ref.1, f32[192,2,768]{2,1,0:T(2,128)} %weight_ref.1, ...), custom_call_target="tpu_custom_call" | custom-call | tf_op jit(solution)/shard_map/pallas_call | solution.py:864
  42.9 1.3 %copy.12 = f32[6,16]{1,0:T(8,128)} copy(f32[6,16]{1,0:T(8,128)} %get-tuple-element.4) | data formatting | bytes 768
  44.2 1.4 %copy.13 = f32[16,768]{1,0:T(8,128)} copy(f32[16,768]{1,0:T(8,128)} %get-tuple-element.5) | data formatting | bytes 98304

commit v5 on v4

--- a/solution.py
+++ b/solution.py
@@ -72,10 +72,12 @@
     rows = own + 2 * side
     dest = destinations(edge_ref, own, side, f_dev, me)
     pick = (iota((rows, edges), 0) == dest).astype(F32).astype(BF16)
-    for tile, copies in enumerate(loads):
+    for tile in range(len(loads)):
         cols = slice(tile * L, (tile + 1) * L)
-        for copy in copies:
-            copy.wait()
+        if tile % 3 == 0:
+            for copies in loads[tile : tile + 3]:
+                for copy in copies:
+                    copy.wait()
         live = mask3[tile].astype(F32)
         fields = []
         for comp in range(2):
@@ -126,8 +128,8 @@
     return [
         h00, h02, x2, x3, x1,
         h11, h12, y3, y2, y1,
-        h02 * u + h12 * v, u * x2 + v * y3, u * x3 + v * y2, u * x1 - v * y1,
-        a2 * uv + b3 * vv, a2 * uu + b3 * uv, a2 * v - b3 * u,
+        h02 * u + h12 * v, u * x2 + v * y3, u * x3 + v * y2, x2 - y2,
+        a2 * uv + b3 * vv, uv * (a3 + b3), a2 * v - b3 * u,
         a3 * uu + b2 * uv, b2 * u - a3 * v,
         a1 * v + b1 * u,
     ]
@@ -194,7 +196,7 @@
     vv = 1.0 + v * v
     uv = u * v
     e = motion_sums(u, v, uu, vv, au, av, ds)
-    back = fold(adj_t(rel, tr, e))
+    back = adj_t(rel, tr, e)
     sums = curvature_sums(u, v, uu, vv, uv, ds, wu, wv) + motion_sums(u, v, uu, vv, gu, gv, ds)
     return e, back, au * su + av * sv, su * gu + sv * gv, sums
 
@@ -254,9 +256,10 @@
                 slot = s * tiles + tile
                 for j in range(6):
                     e_ref[slot, j] = e[j]
-                part_ref[slot, 0] = back
-                part_ref[slot, 1] = curv
-                part_ref[slot, 2] = grad
+                for j in range(6):
+                    part_ref[slot, j] = back[j]
+                part_ref[slot, 6] = curv
+                part_ref[slot, 7] = grad
                 sums = new if sums is None else [a + b for a, b in zip(sums, new)]
             note(lane == s + RADIUS, sums, rel + tr, sum_ref, pair_ref)
 
@@ -317,10 +320,10 @@
                 here = s * tiles + tile
                 for j in range(6):
                     e_ref[here, 6 + j] = e[j]
-                back = -(back + part_ref[here, 0])
+                back = -fold([x + part_ref[here, j] for j, x in enumerate(back)])
                 e_ref[here, 12] = back
-                curv = jnp.sum(curv + part_ref[here, 1], axis=0, keepdims=True) + damp3[tile, pl.ds(s, 1), :]
-                grad = -jnp.sum(grad + part_ref[here, 2], axis=0, keepdims=True)
+                curv = jnp.sum(curv + part_ref[here, 6], axis=0, keepdims=True) + damp3[tile, pl.ds(s, 1), :]
+                grad = -jnp.sum(grad + part_ref[here, 7], axis=0, keepdims=True)
                 inv = 1.0 / curv
                 scale = 1.0 / jnp.sqrt(curv)
                 base_ref[tile, pl.ds(s, 1), :] = grad * inv
@@ -840,7 +843,7 @@
     far = pl.BlockSpec(memory_space=pl.ANY)
     return pl.pallas_call(
         body,
-        out_shape=[jax.ShapeDtypeStruct(s, t) for s, t in out],
+        out_shape=[pltpu.VMEM(s, t) for s, t in out],
         in_specs=[vm] * vmem + [far] * hbm,
         out_specs=[vm] * len(out),
         scratch_shapes=scratch,
@@ -881,7 +884,7 @@
             pltpu.VMEM((tiles, f_dev, L), F32),
             pltpu.VMEM((tiles, f_dev, L), F32),
             pltpu.VMEM((f_dev * tiles, 13, 8, L), F32),
-            pltpu.VMEM((f_dev * tiles, 3, 8, L), F32),
+            pltpu.VMEM((f_dev * tiles, 8, 8, L), F32),
             pltpu.VMEM((sums, 8, L), F32),
             pltpu.VMEM((12, 8, L), F32),
             pltpu.VMEM((sums, 8, L), F32),

time: 46 us -> 43.7 us (0.950)
  local copies, waits for them, and re-layouts: 2.69 us -> 1.21 us
  Pallas kernels: 42.3 us -> 41.5 us
    unnamed x2, local copies, waits for them, and re-layouts: 2.69 us -> 1.21 us
    pallas_call x1, Pallas kernels: 42.3 us -> 41.5 us  [per_device(): call(solve, [((6, f_dev), F32), ((f_dev, pix), F32)], [pltpu.VMEM((tiles,...]
where the time goes in v5:
time: 43.7 us; the launch traced here: 43.4 us
  Pallas kernels  41.5 us (95%)
  local copies, waits for them, and re-layouts  1.21 us (3%)
  between operations  0.64 us (1%)
    pallas_call x1, Pallas kernels, per_device(): call(solve, [((6, f_dev), F32), ((f_dev, pix), F32)], [pltpu.VMEM((tiles,...  41.5 us
    unnamed x2, local copies, waits for them, and re-layouts  1.21 us

profile of v5, /device:TPU:1, one launch (start us, length us, event | category | flops | bytes accessed | tf_op | source)
XLA Modules:
  0.0 43.4 jit_solution(4096863807490044794)
XLA Ops:
  0.6 41.5 %shard_map.95 = (f32[6,16]{1,0:T(8,128)S(1)}, f32[16,768]{1,0:T(8,128)S(1)}) custom-call(s32[2,192]{1,0:T(2,128)} %edge_ref.1, f32[3,128]{1,0:T(4,128)} %rot_ref.1, f32[3,128]{1,0:T(4,128)} %trans_ref.1, f32[16,768]{1,0:T(8,128)} %depth_ref.1, f32[16,768]{1,0:T(8,128)} %damp_ref.1, f32[192,2,768]{2,1,0:T(2,128)} %flow_ref.1, f32[192,2,768]{2,1,0:T(2,128)} %weight_ref.1, ...), custom_call_target="tpu_custom_call" | custom-call | tf_op jit(solution)/shard_map/pallas_call | solution.py:867
  42.2 0.6 %copy.12 = f32[6,16]{1,0:T(8,128)} copy(f32[6,16]{1,0:T(8,128)S(1)} %get-tuple-element.2) | data formatting | bytes 768
  42.8 0.6 %copy.13 = f32[16,768]{1,0:T(8,128)} copy(f32[16,768]{1,0:T(8,128)S(1)} %get-tuple-element.3) | data formatting | bytes 98304

commit v6 on v5

--- a/solution.py
+++ b/solution.py
@@ -65,7 +65,7 @@
     return out
 
 
-def aggregate(edge_ref, loads, flow3, weight3, mask3, own_ref, low_ref, high_ref, me, f_dev):
+def aggregate(edge_ref, loads, flow3, weight3, mask3, own_ref, low_ref, high_ref, me, f_dev, ready):
     edges = edge_ref.shape[1]
     own = own_ref.shape[1]
     side = low_ref.shape[2]
@@ -92,6 +92,8 @@
             own_ref[field, :, cols] = part[:own]
             low_ref[tile, field] = part[own : own + side]
             high_ref[tile, field] = part[own + side :]
+        if tile % 3 == 2 or tile == len(loads) - 1:
+            ready(range(tile - tile % 3, tile + 1))
 
 
 def window(load, me, f_dev, frames):
@@ -751,10 +753,11 @@
     down = [remote(low_out.at[t, :, :SENT], low_ref.at[t, :, :SENT], sems, 0, t, "frames", below) for t in range(tiles)]
     up = [remote(high_out.at[t, :, :SENT], high_ref.at[t, :, :SENT], sems, 1, t, "frames", over) for t in range(tiles)]
 
-    @pl.when(me < count - 1)
-    def _():
-        for copy in up:
-            copy.start()
+    def ascend(span):
+        @pl.when(me < count - 1)
+        def _():
+            for t in span:
+                up[t].start()
 
     def descend():
         @pl.when(me > 0)
@@ -796,7 +799,7 @@
             for copy in up:
                 copy.wait_send()
 
-    return descend, receive, drain
+    return ascend, descend, receive, drain
 
 
 def solve(
@@ -825,9 +828,14 @@
     for k in range(6):
         pose_ref[k] = jnp.broadcast_to(turned[:WIN, k : k + 1], (WIN, L))
     prepare(pose_ref, frame_ref, coord_ref, depth_ref, damp_ref, depth3, damp3)
-    aggregate(edge_ref, loads, flow3, weight3, mask3, own_ref, low_out, high_out, me, f_dev)
-    pl.semaphore_wait(barrier, total)
-    descend, receive, drain = swap_edges(low_out, high_out, low_ref, high_ref, edge_sem)
+    ascend, descend, receive, drain = swap_edges(low_out, high_out, low_ref, high_ref, edge_sem)
+
+    def ready(span):
+        if span[0] == 0:
+            pl.semaphore_wait(barrier, total)
+        ascend(span)
+
+    aggregate(edge_ref, loads, flow3, weight3, mask3, own_ref, low_out, high_out, me, f_dev, ready)
     near_pairs(own_ref, frame_ref, coord_ref, depth3, e_ref, part_ref, near_sum, near_pair, descend)
     far_pairs(
         own_ref, low_ref, high_ref, frame_ref, coord_ref, depth3, damp3, e_ref, part_ref,

time: 43.7 us -> 43.1 us (0.986)
  Pallas kernels: 41.5 us -> 40.9 us
    pallas_call x1, Pallas kernels: 41.5 us -> 40.9 us  [per_device(): call(solve, [((6, f_dev), F32), ((f_dev, pix), F32)], [pltpu.VMEM((tiles,...]
where the time goes in v6:
time: 43.1 us; the launch traced here: 42.8 us
  Pallas kernels  40.9 us (95%)
  local copies, waits for them, and re-layouts  1.21 us (3%)
  between operations  0.64 us (1%)
    pallas_call x1, Pallas kernels, per_device(): call(solve, [((6, f_dev), F32), ((f_dev, pix), F32)], [pltpu.VMEM((tiles,...  40.9 us
    unnamed x2, local copies, waits for them, and re-layouts  1.21 us

profile of v6, /device:TPU:1, one launch (start us, length us, event | category | flops | bytes accessed | tf_op | source)
XLA Modules:
  0.0 42.8 jit_solution(4785191157674094122)
XLA Ops:
  0.6 40.9 %shard_map.95 = (f32[6,16]{1,0:T(8,128)S(1)}, f32[16,768]{1,0:T(8,128)S(1)}) custom-call(s32[2,192]{1,0:T(2,128)} %edge_ref.1, f32[3,128]{1,0:T(4,128)} %rot_ref.1, f32[3,128]{1,0:T(4,128)} %trans_ref.1, f32[16,768]{1,0:T(8,128)} %depth_ref.1, f32[16,768]{1,0:T(8,128)} %damp_ref.1, f32[192,2,768]{2,1,0:T(2,128)} %flow_ref.1, f32[192,2,768]{2,1,0:T(2,128)} %weight_ref.1, ...), custom_call_target="tpu_custom_call" | custom-call | tf_op jit(solution)/shard_map/pallas_call | solution.py:875
  41.5 0.6 %copy.12 = f32[6,16]{1,0:T(8,128)} copy(f32[6,16]{1,0:T(8,128)S(1)} %get-tuple-element.2) | data formatting | bytes 768
  42.1 0.6 %copy.13 = f32[16,768]{1,0:T(8,128)} copy(f32[16,768]{1,0:T(8,128)S(1)} %get-tuple-element.3) | data formatting | bytes 98304

commit v7 on v6

--- a/solution.py
+++ b/solution.py
@@ -554,8 +554,7 @@
     for k in range(4):
         for tile in range(tiles):
             diag_ref[z, k, :, tile * L : (tile + 1) * L] = sums[k][tile]
-    for copy in sent + more:
-        copy.wait_send()
+    pending = sent + more
     mate = me + 1 - 2 * lax.rem(me, 2)
     mine = pl.ds(2 * lax.rem(me, 2), 2)
     half = diag_ref.at[z, mine]
@@ -569,8 +568,7 @@
         passed.append(handed)
     for copy in passed:
         copy.wait_recv()
-    for copy in sent + passed:
-        copy.wait_send()
+    pending = pending + sent + passed
 
     def block(k, at):
         return [
@@ -625,7 +623,7 @@
             at = 6 if i < 4 else 3
             out = jnp.where(row == i, sources[i][t][at : at + 1, :], out)
         rhs.append(out)
-    return rhs, later
+    return rhs, later, pending
 
 
 def conjugate(rhs, later, ahead_ref, back_ref, far_ref):
@@ -706,7 +704,7 @@
     tiles, f_dev = step3.shape[:2]
     half = f_dev // 2
     pack(matrix_ref, packed_ref)
-    rhs, later = operator(
+    rhs, later, pending = operator(
         packed_ref, land, reduced_ref, gathered, diag_ref, ahead_ref, back_ref, far_ref,
         pix_sem, round_sem, mate_sem, f_dev, frames,
     )
@@ -742,6 +740,8 @@
 
     for tile in range(tiles):
         step_ref[:, tile * L : (tile + 1) * L] = step3[tile]
+    for copy in pending:
+        copy.wait_send()
 
 
 def swap_edges(low_out, high_out, low_ref, high_ref, sems):

time: 43.1 us -> 43 us (level)
  no operation moved by 1% of the time
where the time goes in v7:
time: 43 us; the launch traced here: 42.8 us
  Pallas kernels  40.9 us (95%)
  local copies, waits for them, and re-layouts  1.21 us (3%)
  between operations  0.64 us (1%)
    pallas_call x1, Pallas kernels, per_device(): call(solve, [((6, f_dev), F32), ((f_dev, pix), F32)], [pltpu.VMEM((tiles,...  40.9 us
    unnamed x2, local copies, waits for them, and re-layouts  1.21 us

profile of v7, /device:TPU:1, one launch (start us, length us, event | category | flops | bytes accessed | tf_op | source)
XLA Modules:
  0.0 42.8 jit_solution(11421503705100666923)
XLA Ops:
  0.6 40.9 %shard_map.95 = (f32[6,16]{1,0:T(8,128)S(1)}, f32[16,768]{1,0:T(8,128)S(1)}) custom-call(s32[2,192]{1,0:T(2,128)} %edge_ref.1, f32[3,128]{1,0:T(4,128)} %rot_ref.1, f32[3,128]{1,0:T(4,128)} %trans_ref.1, f32[16,768]{1,0:T(8,128)} %depth_ref.1, f32[16,768]{1,0:T(8,128)} %damp_ref.1, f32[192,2,768]{2,1,0:T(2,128)} %flow_ref.1, f32[192,2,768]{2,1,0:T(2,128)} %weight_ref.1, ...), custom_call_target="tpu_custom_call" | custom-call | tf_op jit(solution)/shard_map/pallas_call | solution.py:875
  41.5 0.6 %copy.12 = f32[6,16]{1,0:T(8,128)} copy(f32[6,16]{1,0:T(8,128)S(1)} %get-tuple-element.2) | data formatting | bytes 768
  42.1 0.6 %copy.13 = f32[16,768]{1,0:T(8,128)} copy(f32[16,768]{1,0:T(8,128)S(1)} %get-tuple-element.3) | data formatting | bytes 98304
